TPU v7x, 16 devices: a 4x2x1 block of a 4x4x8 slice. The times are simulated.
16 devices in a mesh: dp: 2 (over y, z), tp: 8 (over x, core).
Axes of the slice: x: 4, y: 2, z: 1, core: 2. Of those that a mesh axis runs over, the one named last changes fastest.
The devices are a block of a 4x4x8 slice.
Arguments:
- x: bfloat16 [256, 4096], P('dp'), parts along dimension 0
- ln_attn_gamma: float32 [4096], replicated
- ln_attn_beta: float32 [4096], replicated
- ln_mlp_gamma: float32 [4096], replicated
- ln_mlp_beta: float32 [4096], replicated
- w_qkv: bfloat16 [4096, 32, 3, 128], P(None, 'tp')
- w_out: bfloat16 [32, 1, 128, 4096], P('tp')
- w_up: bfloat16 [4096, 16384], P(None, 'tp')
- w_down: bfloat16 [16384, 4096], P('tp')
- k_cache: bfloat16 [256, 32, 128, 128], P('dp', 'tp'), parts along dimension 0
- v_cache: bfloat16 [256, 32, 128, 128], P('dp', 'tp'), parts along dimension 0
- positions: int32 [256], P('dp'), parts along dimension 0
Outputs:
- output 1: bfloat16 [256, 4096], P('dp'), parts along dimension 0
- output 2: bfloat16 [256, 32, 128, 128], P('dp', 'tp'), parts along dimension 0
- output 3: bfloat16 [256, 32, 128, 128], P('dp', 'tp'), parts along dimension 0
There are 2 independent parts. A program takes and returns all parts, laid end to end along the dimension named above; an argument that names none is the same for every part.
All inputs are finite; a program needn't handle non-finite values.
Results may differ from a plain program's by a relative error of at most 0.0118648.
Values are sent between devices in bfloat16 or wider.
A program may use at most 768 MiB of HBM per device.

v0:
```python
import jax
import jax.numpy as jnp
from jax import lax
from jax.sharding import PartitionSpec as P

LN_EPS = 1e-5
ROPE_BASE = 10000.0
NEG_BIG = -1e30


def layer_norm(act_rows, ln_gamma, ln_beta):
    rows_f32 = act_rows.astype(jnp.float32)
    row_mean = jnp.mean(rows_f32, axis=-1, keepdims=True)
    centred = rows_f32 - row_mean
    row_var = jnp.mean(centred * centred, axis=-1, keepdims=True)
    return (centred * lax.rsqrt(row_var + LN_EPS) * ln_gamma + ln_beta).astype(jnp.bfloat16)


def apply_rotary(vectors, cos_t, sin_t):
    half_width = vectors.shape[-1] // 2
    as_f32 = vectors.astype(jnp.float32)
    lower_half = as_f32[..., :half_width]
    upper_half = as_f32[..., half_width:]
    return jnp.concatenate([lower_half * cos_t - upper_half * sin_t, upper_half * cos_t + lower_half * sin_t], axis=-1).astype(jnp.bfloat16)


def attend_local(attn_in, w_qkv, k_cache, v_cache, positions):
    n_query = w_qkv.shape[2] - 2
    head_dim = w_qkv.shape[3]
    qkv_rows = jnp.einsum('bd,dgjh->bgjh', attn_in, w_qkv, preferred_element_type=jnp.float32).astype(jnp.bfloat16)
    inv_freq = ROPE_BASE ** (-2.0 * jnp.arange(head_dim // 2, dtype=jnp.float32) / head_dim)
    angles = positions.astype(jnp.float32)[:, None] * inv_freq[None, :]
    cos_t = jnp.cos(angles)
    sin_t = jnp.sin(angles)
    queries = apply_rotary(qkv_rows[:, :, :n_query], cos_t[:, None, None, :], sin_t[:, None, None, :])
    new_key = apply_rotary(qkv_rows[:, :, n_query], cos_t[:, None, :], sin_t[:, None, :])
    new_value = qkv_rows[:, :, n_query + 1]
    slot_ids = jnp.arange(k_cache.shape[2])
    write_mask = (slot_ids[None, :] == positions[:, None])[:, None, :, None]
    keys_all = jnp.where(write_mask, new_key[:, :, None, :], k_cache)
    values_all = jnp.where(write_mask, new_value[:, :, None, :], v_cache)
    valid_mask = (slot_ids[None, :] <= positions[:, None])[:, None, None, :]
    scores = jnp.einsum('bgqh,bgsh->bgqs', queries, keys_all, preferred_element_type=jnp.float32) * (head_dim ** -0.5)
    scores = jnp.where(valid_mask, scores, NEG_BIG)
    attn_probs = jax.nn.softmax(scores, axis=-1).astype(jnp.bfloat16)
    context = jnp.einsum('bgqs,bgsh->bgqh', attn_probs, values_all, preferred_element_type=jnp.float32).astype(jnp.bfloat16)
    return context, keys_all, values_all


def solution(mesh):
    row_spec = P('dp', None)
    vec_spec = P(None)
    cache_spec = P('dp', 'tp', None, None)

    def device_step(x, ln_attn_gamma, ln_attn_beta, ln_mlp_gamma, ln_mlp_beta, w_qkv, w_out, w_up, w_down, k_cache, v_cache, positions):
        attn_in = layer_norm(x, ln_attn_gamma, ln_attn_beta)
        mlp_in = layer_norm(x, ln_mlp_gamma, ln_mlp_beta)
        context, keys_all, values_all = attend_local(attn_in, w_qkv, k_cache, v_cache, positions)
        attn_part = jnp.einsum('bgqh,gqhd->bd', context, w_out, preferred_element_type=jnp.float32).astype(jnp.bfloat16)
        attn_total = lax.psum(attn_part, 'tp')
        hidden = jax.nn.gelu(jnp.dot(mlp_in, w_up, preferred_element_type=jnp.float32), approximate=False).astype(jnp.bfloat16)
        mlp_part = jnp.dot(hidden, w_down, preferred_element_type=jnp.float32).astype(jnp.bfloat16)
        mlp_total = lax.psum(mlp_part, 'tp')
        layer_out = (x.astype(jnp.float32) + attn_total.astype(jnp.float32) + mlp_total.astype(jnp.float32)).astype(jnp.bfloat16)
        return layer_out, keys_all, values_all

    return jax.shard_map(device_step, mesh=mesh, in_specs=(row_spec, vec_spec, vec_spec, vec_spec, vec_spec, P(None, 'tp', None, None), P('tp', None, None, None), P(None, 'tp'), P('tp', None), cache_spec, cache_spec, P('dp')), out_specs=(row_spec, cache_spec, cache_spec), check_vma=False)
```

profile of v0, /device:TPU:113, one launch (start us, length us, event | category | flops | bytes accessed | tf_op | source)
XLA Modules:
  0.0 168.8 jit_solution(10191684647479739681)
XLA Ops:
  7.2 0.1 all-reduce.3.cloned.1.call-start
  7.3 0.7 convert_element_type.65
  7.9 0.7 iota_compare_fusion.1
  8.7 1.5 convert_reduce_fusion
  10.1 1.7 fusion.12
  11.8 0.0 copy-start.3
  11.8 19.9 %copy.22 = bf16[4096,4,3,128]{0,3,2,1:T(8,128)(2,1)} copy(bf16[4096,4,3,128]{3,1,2,0:T(4,128)(2,1)} %param.17) | data formatting | bytes 25165824 | tf_op args[5]
  31.7 6.7 %fusion.25 = f32[128,1536]{0,1:S(1)} fusion(bf16[4096,1536]{0,1:T(8,128)(2,1)} %bitcast.64, bf16[128,4096]{1,0:T(8,128)(2,1)S(1)} %copy-done.1, f32[4096]{0:T(1024)S(1)} %copy-done.2, f32[4096]{0:T(1024)S(1)} %copy-done.3, f32[128]{0:T(128)S(1)} %add_rsqrt_fusion, f32[128]{0:T(128)S(1)} %broadcast_multiply_fusion), kind=kOutput, calls=%fused_computation.32 | convolution fusion | flops 1613758464 | bytes 14451712
  38.4 0.1 convert_element_type.63
  38.5 0.1 fusion.70
  38.5 0.2 multiply_cosine_fusion
  38.9 0.1 copy.27
  39.0 0.2 copy.29
  39.2 0.1 copy.28
  39.4 23.3 %broadcast_select_fusion.1 = (bf16[128,4,128,128]{3,2,1,0:T(8,128)(2,1)}, bf16[128,4,128,128]{3,2,1,0:T(8,128)(2,1)}) fusion(bf16[128,4,128,128]{3,2,1,0:T(8,128)(2,1)} %param.21, pred[128,128]{1,0:T(8,128)(4,1)S(1)} %get-tuple-element.16, bf16[128,4,128]{2,1,0:T(4,128)(2,1)S(1)} %copy.27, bf16[128,4,128,128]{3,2,1,0:T(8,128)(2,1)} %param.22, ...), kind=kLoop, calls=%fused_computation.3 | loop fusion | flops 16777216 | bytes 67387392 | tf_op jit(solution)/shard_map/jit(_where)/select_n | solution.py:40
  62.6 12.2 %fusion.119 = f32[128,4,1,128]{3,2,1,0:T(1,128)S(1)} fusion(bf16[128,4,128,1]{2,3,1,0:T(2,128)(2,1)S(1)} %copy.29, bf16[128,4,128,128]{3,2,1,0:T(8,128)(2,1)} %get-tuple-element.11), kind=kOutput, calls=%fused_computation.143 | convolution fusion | flops 16777216 | bytes 17170432 | tf_op jit(solution)/shard_map/bgqh,bgsh->bgqs/dot_general | solution.py:43
  74.8 0.3 fusion.19
  75.1 0.0 copy-start
  75.1 8.2 %fusion.66 = bf16[128,4,1,128]{3,2,1,0:T(2,128)(2,1)S(1)} fusion(bf16[128,4,128,128]{3,2,1,0:T(8,128)(2,1)} %get-tuple-element.12, bf16[128,4,128,1]{2,0,1,3:T(8,128)(2,1)S(1)} %fusion.19), kind=kOutput, calls=%fused_computation.78 | convolution fusion | flops 16777216 | bytes 17039360 | tf_op jit(solution)/shard_map/bgqs,bgsh->bgqh/dot_general | solution.py:46
  83.3 1.7 %fusion.2 = bf16[128,4096]{1,0:T(8,128)(2,1)} fusion(bf16[4,1,128,4096]{3,2,1,0:T(8,128)(2,1)S(1)} %copy-done, bf16[128,4,1,128]{3,2,1,0:T(2,128)(2,1)S(1)} %fusion.66), kind=kOutput, calls=%fused_computation.6 | convolution fusion | flops 537395200 | bytes 5373952 | tf_op jit(solution)/shard_map/bgqh,gqhd->bd/dot_general | solution.py:59
  85.0 15.2 %convolution_convert_fusion = bf16[128,4096]{1,0:T(8,128)(2,1)} fusion(bf16[2048,4096]{1,0:T(8,128)(2,1)} %param.20, bf16[4096,2048]{1,0:T(8,128)(2,1)} %param.19, bf16[128,4096]{1,0:T(8,128)(2,1)S(1)} %copy-done.1, f32[4096]{0:T(1024)S(1)} %copy-done.4, f32[4096]{0:T(1024)S(1)} %copy-done.5, f32[128]{0:T(128)S(1)} %add_rsqrt_fusion, ...), kind=kOutput, calls=%fused_computation.5 | convolution fusion | flops 4315676672 | bytes 35685376 | tf_op jit(solution)/shard_map/dot_general | solution.py:62
  100.3 0.1 all-reduce.3.cloned.1.call-update
  100.4 58.6 %all-reduce.3.cloned.1.call-done = (bf16[128,4096]{1,0:T(8,128)(2,1)}, bf16[128,4096]{1,0:T(8,128)(2,1)}) async-done(((bf16[128,4096]{1,0:T(8,128)(2,1)}, bf16[128,4096]{1,0:T(8,128)(2,1)}), (bf16[128,4096]{1,0:T(8,128)(2,1)}, bf16[128,4096]{1,0:T(8,128)(2,1)})) %all-reduce.3.cloned.1.call-update) | async-done | bytes 2097168 | tf_op jit(solution)/shard_map/psum | solution.py:63
  159.0 3.0 %fusion.14 = bf16[128,4096]{1,0:T(8,128)(2,1)} fusion(bf16[128,4096]{1,0:T(8,128)(2,1)S(1)} %copy-done.1, bf16[128,4096]{1,0:T(8,128)(2,1)} %get-tuple-element.3, bf16[128,4096]{1,0:T(8,128)(2,1)} %get-tuple-element.4), kind=kLoop, calls=%fused_computation.21 | loop fusion | flops 3145728 | bytes 4194304 | tf_op jit(solution)/shard_map/convert_element_type | solution.py:64
  (18 shorter events, 0.2 us)
Async XLA Ops:
  7.2 151.8 %all-reduce.3.cloned.1.call-start = ((), (), s32[]{:S(2)}) async-start(), calls=%async_computation | async-start | bytes 4194304 | tf_op jit(solution)/shard_map/psum | solution.py:63
  11.8 19.9 %copy-start.1 = (bf16[128,4096]{1,0:T(8,128)(2,1)S(1)}, bf16[128,4096]{1,0:T(8,128)(2,1)}, u32[]{:S(2)}) copy-start(bf16[128,4096]{1,0:T(8,128)(2,1)} %param.12) | copy-start | bytes 3145732
  11.8 19.9 %copy-start.2 = (f32[4096]{0:T(1024)S(1)}, f32[4096]{0:T(1024)}, u32[]{:S(2)}) copy-start(f32[4096]{0:T(1024)} %param.14) | copy-start | bytes 49156
  11.8 19.9 %copy-start.3 = (f32[4096]{0:T(1024)S(1)}, f32[4096]{0:T(1024)}, u32[]{:S(2)}) copy-start(f32[4096]{0:T(1024)} %param.13) | copy-start | bytes 49156
  75.1 8.2 %copy-start = (bf16[4,1,128,4096]{3,2,1,0:T(8,128)(2,1)S(1)}, bf16[4,1,128,4096]{3,2,1,0:T(8,128)(2,1)}, u32[]{:S(2)}) copy-start(bf16[4,1,128,4096]{3,2,1,0:T(8,128)(2,1)} %param.18) | copy-start | bytes 12582916
  83.3 1.7 %copy-start.4 = (f32[4096]{0:T(1024)S(1)}, f32[4096]{0:T(1024)}, u32[]{:S(2)}) copy-start(f32[4096]{0:T(1024)} %param.16) | copy-start | bytes 49156
  83.3 1.7 %copy-start.5 = (f32[4096]{0:T(1024)S(1)}, f32[4096]{0:T(1024)}, u32[]{:S(2)}) copy-start(f32[4096]{0:T(1024)} %param.15) | copy-start | bytes 49156
Sparse Core Ops, SparseCore 0:
  100.5 58.4 all-reduce.2
where the time goes:
time: 171 us; the launch traced here: 169 us
  waiting for transfers between devices  58.7 us (34%)
  matrix products  44 us (26%)
  other arithmetic  31.5 us (18%)
  local copies, waits for them, and re-layouts  20.4 us (12%)
  between operations  14.2 us (8%)
    psum x1, waiting for transfers between devices, device_step(): mlp_total = lax.psum(mlp_part, 'tp')  58.6 us
    select_n x1, other arithmetic, attend_local(): keys_all = jnp.where(write_mask, new_key[:, :, None, :], k_cache)  23.3 us
    unnamed x13, local copies, waits for them, and re-layouts  19.9 us
    dot_general x1, matrix products, device_step(): jnp.dot(hidden, w_down, preferred_element_type=jnp.float32)  15.2 us
    dot_general x1, matrix products, attend_local(): jnp.einsum('bgqh,bgsh->bgqs', queries, keys_all, preferred_element_type=j...  12.2 us
    dot_general x1, matrix products, attend_local(): jnp.einsum('bgqs,bgsh->bgqh', attn_probs, values_all, preferred_element_t...  8.21 us
    unnamed x1, matrix products  6.66 us
  transfers between devices with their start and end apart: 1, of which 1 were waited for; matrix products, arithmetic and copies ran while one was open for 0% of the time, Pallas kernels for 0%

commit v1 on v0

v1 whole, which is shorter than its diff:
```python
import functools

import jax
import jax.numpy as jnp
from jax import lax
from jax.experimental import pallas as pl
from jax.experimental.pallas import tpu as pltpu
from jax.sharding import PartitionSpec as P

LN_EPS = 1e-5
ROPE_BASE = 10000.0
NEG_BIG = -1e30
LANES = 128
ROWS_PER_CHUNK = 8
W_CHUNK = 256
F32 = jnp.float32
BF16 = jnp.bfloat16
ANY = pl.BlockSpec(memory_space=pl.ANY)
VMEM = pl.BlockSpec(memory_space=pltpu.VMEM)
SMEM = pl.BlockSpec(memory_space=pltpu.SMEM)


def norm_into(x_ref, gamma_ref, beta_ref, dst_ref):
    rows, width = x_ref.shape
    tiles = width // LANES

    def tile(c):
        return x_ref[:, pl.ds(pl.multiple_of(c * LANES, LANES), LANES)].astype(F32)

    zero = jnp.zeros((rows, LANES), F32)
    total = lax.fori_loop(0, tiles, lambda c, s: s + tile(c), zero, unroll=4)
    mean = jnp.sum(total, axis=-1, keepdims=True) / width

    def square(c, s):
        d = tile(c) - mean
        return s + d * d

    var = jnp.sum(lax.fori_loop(0, tiles, square, zero, unroll=4), axis=-1, keepdims=True) / width
    inv = lax.rsqrt(var + LN_EPS)

    def write(c, carry):
        y = (tile(c) - mean) * inv * gamma_ref[pl.ds(c, 1), :] + beta_ref[pl.ds(c, 1), :]
        dst_ref[:, pl.ds(pl.multiple_of(c * LANES, LANES), LANES)] = y.astype(BF16)
        return carry

    lax.fori_loop(0, tiles, write, 0, unroll=4)


def attention_kernel(pos_ref, x_ref, gamma_ref, beta_ref, cos_ref, sin_ref, w_ref, k_ref, v_ref, ctx_ref, ko_ref, vo_ref,
                     wbuf, wf, acc, attn, q_s, kn_s, vn_s, kbuf, vbuf, wsem, insem, outsem):
    rows, width = x_ref.shape
    _, groups, slots, head = k_ref.shape
    cols = 3 * groups
    n_w = width // W_CHUNK
    n_c = rows // ROWS_PER_CHUNK
    wrows = W_CHUNK * cols

    def w_copy(c):
        at = pl.ds(pl.multiple_of(c * wrows, wrows), wrows)
        return pltpu.make_async_copy(w_ref.at[at], wbuf.at[at], wsem.at[c])

    def io(i, which, out):
        hbm_in, hbm_out, buf = ((k_ref, ko_ref, kbuf), (v_ref, vo_ref, vbuf))[which]
        at = pl.ds(i * ROWS_PER_CHUNK, ROWS_PER_CHUNK)
        if out:
            return pltpu.make_async_copy(buf.at[at], hbm_out.at[at], outsem.at[which, i])
        return pltpu.make_async_copy(hbm_in.at[at], buf.at[at], insem.at[which, i])

    for c in range(n_w):
        w_copy(c).start()
    for i in range(n_c):
        io(i, 0, False).start()
        io(i, 1, False).start()

    norm_into(x_ref, gamma_ref, beta_ref, attn)
    acc[...] = jnp.zeros_like(acc)

    def project(c, carry):
        w_copy(c).wait()
        wf[...] = wbuf[pl.ds(pl.multiple_of(c * wrows, wrows), wrows), :].astype(F32)
        lhs = attn[:, pl.ds(pl.multiple_of(c * W_CHUNK, W_CHUNK), W_CHUNK)]
        for n in range(0, cols, 2):
            rhs = jnp.concatenate(
                [wf[pl.ds(n + e, W_CHUNK, stride=cols), :].astype(BF16) for e in range(2)], axis=1)
            acc[:, n * head:(n + 2) * head] += jnp.dot(lhs, rhs, preferred_element_type=F32)
        return carry

    lax.fori_loop(0, n_w, project, 0)

    cos_t, sin_t = cos_ref[...], sin_ref[...]

    def rotate(u):
        u = u.astype(BF16).astype(F32)
        return (u * cos_t + pltpu.roll(u, head // 2, 1) * sin_t).astype(BF16).astype(F32)

    for g in range(groups):
        at = pl.ds(g, rows, stride=groups)
        q_s[at, :] = rotate(acc[:, g * head:(g + 1) * head])
        kn_s[at, :] = rotate(acc[:, (groups + g) * head:(groups + g + 1) * head])
        vn_s[at, :] = acc[:, (2 * groups + g) * head:(2 * groups + g + 1) * head].astype(BF16).astype(F32)

    row16 = lax.broadcasted_iota(jnp.int32, (16, head), 0)
    row8 = lax.broadcasted_iota(jnp.int32, (2 * groups, slots), 0)
    lane8 = lax.broadcasted_iota(jnp.int32, (2 * groups, slots), 1)
    scale = head ** -0.5

    def chunk(i, carry):
        io(i, 0, False).wait()
        io(i, 1, False).wait()

        def write_row(r, carry):
            b = i * ROWS_PER_CHUNK + r
            pos = pos_ref[b]
            base = pl.multiple_of((pos // 16) * 16, 16)
            hit = row16 == pos - base
            for g in range(groups):
                for buf, new in ((kbuf, kn_s), (vbuf, vn_s)):
                    old = buf[b, g, pl.ds(base, 16), :].astype(F32)
                    row = new[pl.ds(b * groups + g, 1), :]
                    buf[b, g, pl.ds(base, 16), :] = jnp.where(hit, row, old).astype(BF16)
            return carry

        lax.fori_loop(0, ROWS_PER_CHUNK, write_row, 0, unroll=True)
        io(i, 0, True).start()
        io(i, 1, True).start()

        for pair in range(ROWS_PER_CHUNK // 2):
            b = i * ROWS_PER_CHUNK + 2 * pair
            at = pl.ds(pl.multiple_of(b * groups, 2 * groups), 2 * groups)
            q8 = q_s[at, :].astype(BF16)
            keys = kbuf[pl.ds(b, 2)].reshape(2 * groups * slots, head)
            every = lax.dot_general(q8, keys, (((1,), (1,)), ((), ())), preferred_element_type=F32)
            s = every[:, 0:slots]
            for t in range(1, 2 * groups):
                s = jnp.where(row8 == t, every[:, t * slots:(t + 1) * slots], s)
            pos8 = jnp.where(row8 < groups, pos_ref[b], pos_ref[b + 1])
            s = jnp.where(lane8 <= pos8, s * scale, NEG_BIG)
            e = jnp.exp(s - jnp.max(s, axis=-1, keepdims=True))
            p = e / jnp.sum(e, axis=-1, keepdims=True)
            spread = jnp.concatenate([jnp.where(row8 == t, p, 0.0) for t in range(2 * groups)], axis=1).astype(BF16)
            values = vbuf[pl.ds(b, 2)].reshape(2 * groups * slots, head)
            ctx_ref[at, :] = jnp.dot(spread, values, preferred_element_type=F32).astype(BF16).astype(F32)
        return carry

    lax.fori_loop(0, n_c, chunk, 0)
    for i in range(n_c):
        io(i, 0, True).wait()
        io(i, 1, True).wait()


def attend(x, gamma, beta, w_qkv, k_cache, v_cache, positions):
    rows, width = x.shape
    _, groups, slots, head = k_cache.shape
    cols = 3 * groups
    inv_freq = ROPE_BASE ** (-2.0 * jnp.arange(head // 2, dtype=F32) / head)
    angles = positions.astype(F32)[:, None] * inv_freq[None, :]
    cos_t, sin_t = jnp.cos(angles), jnp.sin(angles)
    cos_t = jnp.concatenate([cos_t, cos_t], axis=1)
    sin_t = jnp.concatenate([-sin_t, sin_t], axis=1)
    w_rows = jnp.transpose(w_qkv, (0, 2, 1, 3)).reshape(width * cols, head)
    n_w, n_c = width // W_CHUNK, rows // ROWS_PER_CHUNK
    return pl.pallas_call(
        attention_kernel,
        out_shape=[jax.ShapeDtypeStruct((rows * groups, head), F32),
                   jax.ShapeDtypeStruct(k_cache.shape, k_cache.dtype),
                   jax.ShapeDtypeStruct(v_cache.shape, v_cache.dtype)],
        in_specs=[SMEM, VMEM, VMEM, VMEM, VMEM, VMEM, ANY, ANY, ANY],
        out_specs=[VMEM, ANY, ANY],
        scratch_shapes=[
            pltpu.VMEM((width * cols, head), BF16),
            pltpu.VMEM((W_CHUNK * cols, head), F32),
            pltpu.VMEM((rows, cols * head), F32),
            pltpu.VMEM((rows, width), BF16),
            pltpu.VMEM((rows * groups, head), F32),
            pltpu.VMEM((rows * groups, head), F32),
            pltpu.VMEM((rows * groups, head), F32),
            pltpu.VMEM(k_cache.shape, BF16),
            pltpu.VMEM(v_cache.shape, BF16),
            pltpu.SemaphoreType.DMA((n_w,)),
            pltpu.SemaphoreType.DMA((2, n_c)),
            pltpu.SemaphoreType.DMA((2, n_c)),
        ],
        compiler_params=pltpu.CompilerParams(vmem_limit_bytes=60 * 1024 * 1024),
        name='attend',
    )(positions, x, gamma.reshape(-1, LANES), beta.reshape(-1, LANES), cos_t, sin_t, w_rows, k_cache, v_cache)


def layer_norm(act_rows, ln_gamma, ln_beta):
    rows_f32 = act_rows.astype(jnp.float32)
    row_mean = jnp.mean(rows_f32, axis=-1, keepdims=True)
    centred = rows_f32 - row_mean
    row_var = jnp.mean(centred * centred, axis=-1, keepdims=True)
    return (centred * lax.rsqrt(row_var + LN_EPS) * ln_gamma + ln_beta).astype(jnp.bfloat16)


def solution(mesh):
    row_spec = P('dp', None)
    vec_spec = P(None)
    cache_spec = P('dp', 'tp', None, None)

    def device_step(x, ln_attn_gamma, ln_attn_beta, ln_mlp_gamma, ln_mlp_beta, w_qkv, w_out, w_up, w_down, k_cache, v_cache, positions):
        mlp_in = layer_norm(x, ln_mlp_gamma, ln_mlp_beta)
        context, keys_all, values_all = attend(x, ln_attn_gamma, ln_attn_beta, w_qkv, k_cache, v_cache, positions)
        rows = x.shape[0]
        context = context.astype(BF16).reshape(rows, -1)
        attn_part = jnp.dot(context, w_out.reshape(-1, x.shape[1]), preferred_element_type=jnp.float32)
        hidden = jax.nn.gelu(jnp.dot(mlp_in, w_up, preferred_element_type=jnp.float32), approximate=False).astype(jnp.bfloat16)
        mlp_part = jnp.dot(hidden, w_down, preferred_element_type=jnp.float32)
        total = lax.psum((attn_part + mlp_part).astype(BF16), 'tp')
        layer_out = (x.astype(jnp.float32) + total.astype(jnp.float32)).astype(jnp.bfloat16)
        return layer_out, keys_all, values_all

    return jax.shard_map(device_step, mesh=mesh, in_specs=(row_spec, vec_spec, vec_spec, vec_spec, vec_spec, P(None, 'tp', None, None), P('tp', None, None, None), P(None, 'tp'), P('tp', None), cache_spec, cache_spec, P('dp')), out_specs=(row_spec, cache_spec, cache_spec), check_vma=False)
```

time: 171 us -> 143 us (0.84)
  Pallas kernels: 0 us -> 44.5 us
  matrix products: 44 us -> 18.3 us
  other arithmetic: 31.5 us -> 8.27 us
  local copies, waits for them, and re-layouts: 20.4 us -> 0.1 us
  waiting for transfers between devices: 58.7 us -> 55.4 us
    pallas_call x0 -> x1, Pallas kernels: none -> 44.5 us  [attend(): pl.pallas_call(attention_kernel, out_shape=[jax.ShapeDtypeStruct((rows *...]
    select_n x1 -> x0, other arithmetic: 23.3 us -> none  [attend_local(): keys_all = jnp.where(write_mask, new_key[:, :, None, :], k_cache)]
    unnamed x13 -> x6, local copies, waits for them, and re-layouts: 19.9 us -> 0.01 us
    dot_general x4 -> x2, matrix products: 37.4 us -> 18.3 us  [the longest x1 14.3 us: device_step(): mlp_part = jnp.dot(hidden, w_down, preferred_element_type=jnp.float32)]
    unnamed x1 -> x0, matrix products: 6.66 us -> none
    psum x1, waiting for transfers between devices: 58.6 us -> 55.3 us  [device_step(): total = lax.psum((attn_part + mlp_part).astype(BF16), 'tp')]
    convert_element_type x4 -> x3, other arithmetic: 3.77 us -> 4.07 us  [the longest x1 2.44 us: device_step(): (x.astype(jnp.float32) + total.astype(jnp.float32)).astype(jnp.bfloat16)]
where the time goes in v1:
time: 143 us; the launch traced here: 141 us
  waiting for transfers between devices  55.4 us (39%)
  Pallas kernels  44.5 us (31%)
  matrix products  18.3 us (13%)
  between operations  14.1 us (10%)
  other arithmetic  8.27 us (6%)
    psum x1, waiting for transfers between devices, device_step(): total = lax.psum((attn_part + mlp_part).astype(BF16), 'tp')  55.3 us
    pallas_call x1, Pallas kernels, attend(): pl.pallas_call(attention_kernel, out_shape=[jax.ShapeDtypeStruct((rows *...  44.5 us
    dot_general x1, matrix products, device_step(): mlp_part = jnp.dot(hidden, w_down, preferred_element_type=jnp.float32)  14.3 us
    dot_general x1, matrix products, device_step(): jnp.dot(context, w_out.reshape(-1, x.shape[1]), preferred_element_type=jn...  4.01 us
  transfers between devices with their start and end apart: 1, of which 1 were waited for; matrix products, arithmetic and copies ran while one was open for 0% of the time, Pallas kernels for 0%

profile of v1, /device:TPU:113, one launch (start us, length us, event | category | flops | bytes accessed | tf_op | source)
XLA Modules:
  0.0 140.7 jit_solution(14150206698414482191)
XLA Ops:
  7.2 0.1 all-reduce.2.cloned.1.call-start
  7.3 0.7 convert_element_type.26
  7.9 1.5 %convert_reduce_fusion = f32[128]{0:T(128)S(1)} fusion(bf16[128,4096]{1,0:T(8,128)(2,1)} %x_ref.1), kind=kLoop, calls=%fused_computation.4 | loop fusion | flops 1048448 | bytes 1049088 | tf_op jit(solution)/shard_map/reduce_sum | solution.py:190
  9.4 1.7 %fusion.3 = f32[128]{0:T(128)S(1)} fusion(bf16[128,4096]{1,0:T(8,128)(2,1)} %x_ref.1, f32[128]{0:T(128)S(1)} %broadcast_multiply_fusion), kind=kLoop, calls=%fused_computation.7 | loop fusion | flops 2097024 | bytes 1049600 | tf_op jit(solution)/shard_map/reduce_sum | solution.py:192
  11.0 0.3 fusion.59
  11.4 0.8 pad_maximum_fusion
  12.1 0.0 copy-start
  12.1 0.0 copy-start.1
  12.1 0.0 copy-start.2
  12.1 44.5 %attend.1 = (f32[512,128]{1,0:T(8,128)}, bf16[128,4,128,128]{3,2,1,0:T(8,128)(2,1)}, bf16[128,4,128,128]{3,2,1,0:T(8,128)(2,1)}) custom-call(s32[128]{0:T(128)} %pos_ref.1, bf16[128,4096]{1,0:T(8,128)(2,1)} %x_ref.1, f32[32,128]{1,0:T(8,128)} %bitcast.12, f32[32,128]{1,0:T(8,128)} %bitcast.13, f32[128,128]{1,0:T(8,128)} %get-tuple-element.12.cos_ref, ...), custom_call_target="tpu_custom_call" | custom-call | tf_op jit(solution)/shard_map/attend/pallas_call | solution.py:162
  56.6 1.0 convert_element_type.27
  57.6 0.1 reshape.44
  57.7 0.0 copy-done
  57.7 0.0 copy-done.1
  57.7 0.0 copy-done.2
  57.7 14.3 %fusion.27 = f32[128,4096]{1,0:T(8,128)S(1)} fusion(bf16[2048,4096]{1,0:T(8,128)(2,1)} %param.20, bf16[4096,2048]{1,0:T(8,128)(2,1)} %param.19, bf16[128,4096]{1,0:T(8,128)(2,1)S(1)} %copy-done, f32[4096]{0:T(1024)S(1)} %copy-done.1, f32[4096]{0:T(1024)S(1)} %copy-done.2, f32[128]{0:T(128)S(1)} %add_rsqrt_fusion, f32[128]{0:T(128)S(1)} %broadcast_multiply_fusion), kind=kOutput, calls=%fused_computation.36 | convolution fusion | flops 4315152384 | bytes 36733952 | tf_op jit(solution)/shard_map/dot_general | solution.py:208
  72.0 4.0 %fusion = bf16[128,4096]{1,0:T(8,128)(2,1)} fusion(f32[128,4096]{1,0:T(8,128)S(1)} %fusion.27, bf16[128,512]{1,0:T(8,128)(2,1)S(1)} %reshape.44, bf16[512,4096]{1,0:T(8,128)(2,1)} %bitcast.11), kind=kOutput, calls=%fused_computation.1 | convolution fusion | flops 537919488 | bytes 7471104 | tf_op jit(solution)/shard_map/dot_general | solution.py:206
  76.0 0.1 all-reduce.2.cloned.1.call-update
  76.1 55.3 %all-reduce.2.cloned.1.call-done = bf16[128,4096]{1,0:T(8,128)(2,1)} async-done(((bf16[128,4096]{1,0:T(8,128)(2,1)}), bf16[128,4096]{1,0:T(8,128)(2,1)}) %all-reduce.2.cloned.1.call-update) | async-done | bytes 1048592 | tf_op jit(solution)/shard_map/psum | solution.py:209
  131.4 2.4 %fusion.7 = bf16[128,4096]{1,0:T(8,128)(2,1)} fusion(bf16[128,4096]{1,0:T(8,128)(2,1)S(1)} %copy-done, bf16[128,4096]{1,0:T(8,128)(2,1)} %all-reduce.2.cloned.1.call-done), kind=kLoop, calls=%fused_computation.11 | loop fusion | flops 2097152 | bytes 3145728 | tf_op jit(solution)/shard_map/convert_element_type | solution.py:210
  (3 shorter events, 0.0 us)
Async XLA Ops:
  7.2 124.2 %all-reduce.2.cloned.1.call-start = ((), (), s32[]{:S(2)}) async-start(), calls=%async_computation | async-start | bytes 2097152 | tf_op jit(solution)/shard_map/psum | solution.py:209
  12.1 45.5 %copy-start = (bf16[128,4096]{1,0:T(8,128)(2,1)S(1)}, bf16[128,4096]{1,0:T(8,128)(2,1)}, u32[]{:S(2)}) copy-start(bf16[128,4096]{1,0:T(8,128)(2,1)} %x_ref.1) | copy-start | bytes 3145732
  12.1 45.5 %copy-start.1 = (f32[4096]{0:T(1024)S(1)}, f32[4096]{0:T(1024)}, u32[]{:S(2)}) copy-start(f32[4096]{0:T(1024)} %param.16) | copy-start | bytes 49156
  12.1 45.6 %copy-start.2 = (f32[4096]{0:T(1024)S(1)}, f32[4096]{0:T(1024)}, u32[]{:S(2)}) copy-start(f32[4096]{0:T(1024)} %param.15) | copy-start | bytes 49156
Sparse Core Ops, SparseCore 0:
  76.2 55.1 all-reduce.1

commit v2 on v1

--- a/solution.py
+++ b/solution.py
@@ -1,5 +1,3 @@
-import functools
-
 import jax
 import jax.numpy as jnp
 from jax import lax
@@ -13,11 +11,14 @@
 LANES = 128
 ROWS_PER_CHUNK = 8
 W_CHUNK = 256
+UP_COLS = 512
+OUT_COLS = 512
 F32 = jnp.float32
 BF16 = jnp.bfloat16
 ANY = pl.BlockSpec(memory_space=pl.ANY)
 VMEM = pl.BlockSpec(memory_space=pltpu.VMEM)
 SMEM = pl.BlockSpec(memory_space=pltpu.SMEM)
+MESH = pl.DeviceIdType.MESH
 
 
 def norm_into(x_ref, gamma_ref, beta_ref, dst_ref):
@@ -185,12 +186,198 @@
     )(positions, x, gamma.reshape(-1, LANES), beta.reshape(-1, LANES), cos_t, sin_t, w_rows, k_cache, v_cache)
 
 
-def layer_norm(act_rows, ln_gamma, ln_beta):
-    rows_f32 = act_rows.astype(jnp.float32)
-    row_mean = jnp.mean(rows_f32, axis=-1, keepdims=True)
-    centred = rows_f32 - row_mean
-    row_var = jnp.mean(centred * centred, axis=-1, keepdims=True)
-    return (centred * lax.rsqrt(row_var + LN_EPS) * ln_gamma + ln_beta).astype(jnp.bfloat16)
+def mlp_kernel(x_ref, gamma_ref, beta_ref, ctx_ref, wo_ref, wu_ref, wd_ref, out_ref,
+               wub, wdb, wob, mlp_in, hid, ctxb, part, d2d_src, d2d_dst, cs32, csb, relay_a, relay_b, comb_a, comb_b,
+               from_l, from_r, outb, usem, dsem, osem, send, recv, stored):
+    n_u, _, cu = wub.shape
+    n_b, _, cb = wdb.shape
+    half, slab = d2d_src.shape[1], relay_a.shape[1]
+    chips = half // slab
+    groups = ctxb.shape[1] // LANES
+    rows = x_ref.shape[0]
+    me = lax.axis_index('tp')
+    p, c = lax.div(me, 2), lax.rem(me, 2)
+    right = 2 * lax.rem(p + 1, chips) + c
+    left = 2 * lax.rem(p + chips - 1, chips) + c
+    partner = me + 1 - 2 * c
+    lo, hi = pl.ds(0, cb // 2), pl.ds(cb // 2, cb // 2)
+
+    def up_copy(u):
+        return pltpu.make_async_copy(wu_ref.at[:, pl.ds(u * cu, cu)], wub.at[u], usem.at[u])
+
+    def down_copy(j):
+        return pltpu.make_async_copy(wd_ref.at[:, pl.ds(j * cb, cb)], wdb.at[j], dsem.at[j])
+
+    def out_copy(j):
+        return pltpu.make_async_copy(wo_ref.at[:, pl.ds(j * cb, cb)], wob.at[j], osem.at[j])
+
+    for u in range(n_u):
+        up_copy(u).start()
+    for j in range(n_b):
+        out_copy(j).start()
+        down_copy(j).start()
+
+    barrier = pltpu.get_barrier_semaphore()
+    for peer in (right, left, partner):
+        pl.semaphore_signal(barrier, inc=1, device_id={'tp': peer}, device_id_type=MESH)
+
+    def in_half(q):
+        return pl.ds(pl.multiple_of(lax.rem(p + q, chips) * slab, slab), slab)
+
+    def in_rows(q, core):
+        return pl.ds(pl.multiple_of(core * half + lax.rem(p + q, chips) * slab, slab), slab)
+
+    def remote(kind, j):
+        mine, before, after, far = (in_rows(q, c) for q in (0, chips - 1, 1, 2))
+        src, dst, peer = (
+            (d2d_src.at[j], d2d_dst.at[j], partner),
+            (csb.at[j, in_half(2), lo], relay_a.at[j], right),
+            (csb.at[j, in_half(2), hi], relay_b.at[j], left),
+            (csb.at[j, in_half(1), hi], from_l.at[j, :, hi], right),
+            (csb.at[j, in_half(chips - 1), lo], from_r.at[j, :, lo], left),
+            (comb_a.at[j], from_l.at[j, :, lo], right),
+            (comb_b.at[j], from_r.at[j, :, hi], left),
+            (outb.at[j, mine], outb.at[j, mine], right),
+            (outb.at[j, mine], outb.at[j, mine], left),
+            (outb.at[j, mine], outb.at[j, mine], partner),
+            (outb.at[j, before, lo], outb.at[j, before, lo], right),
+            (outb.at[j, after, hi], outb.at[j, after, hi], left),
+            (outb.at[j, before], outb.at[j, before], partner),
+            (outb.at[j, after], outb.at[j, after], partner),
+            (outb.at[j, far], outb.at[j, far], partner),
+        )[kind]
+        return pltpu.make_async_remote_copy(src_ref=src, dst_ref=dst, send_sem=send.at[kind, j], recv_sem=recv.at[kind, j],
+                                            device_id={'tp': peer}, device_id_type=MESH)
+
+    norm_into(x_ref, gamma_ref, beta_ref, mlp_in)
+    for g in range(groups):
+        ctxb[:, g * LANES:(g + 1) * LANES] = ctx_ref[pl.ds(g, rows, stride=groups), :].astype(BF16)
+
+    def up(u, carry):
+        up_copy(u).wait()
+        z = jnp.dot(mlp_in[...], wub[u], preferred_element_type=F32)
+        hid[u] = (0.5 * z * (1.0 + lax.erf(z * 0.5 ** 0.5))).astype(BF16)
+        return carry
+
+    lax.fori_loop(0, n_u, up, 0)
+    pl.semaphore_wait(barrier, 3)
+
+    own_half = pl.ds(pl.multiple_of(c * half, half), half)
+    other_half = pl.ds(pl.multiple_of((1 - c) * half, half), half)
+
+    def compute(j):
+        out_copy(j).wait()
+        y = jnp.dot(ctxb[...], wob[j], preferred_element_type=F32)
+        down_copy(j).wait()
+        for u in range(n_u):
+            y += jnp.dot(hid[u], wdb[j, u * cu:(u + 1) * cu, :], preferred_element_type=F32)
+        part[j] = y
+        d2d_src[j] = part[j, other_half].astype(BF16)
+        remote(0, j).start()
+
+    def chip_sum(j):
+        remote(0, j).wait_recv()
+        y = part[j, own_half] + d2d_dst[j].astype(F32)
+        cs32[j] = y
+        csb[j] = y.astype(BF16)
+        for kind in (1, 2, 3, 4):
+            remote(kind, j).start()
+
+    def combine(j):
+        remote(1, j).wait_recv()
+        comb_a[j] = (cs32[j, in_half(1), lo] + relay_a[j].astype(F32)).astype(BF16)
+        remote(5, j).start()
+        remote(2, j).wait_recv()
+        comb_b[j] = (cs32[j, in_half(chips - 1), hi] + relay_b[j].astype(F32)).astype(BF16)
+        remote(6, j).start()
+
+    def finish(j):
+        for kind in (3, 4, 5, 6):
+            remote(kind, j).wait_recv()
+        mine = in_rows(0, c)
+        y = cs32[j, in_half(0)] + from_l[j].astype(F32) + from_r[j].astype(F32)
+        outb[j, mine] = (x_ref[mine, j * cb:(j + 1) * cb].astype(F32) + y).astype(BF16)
+        for kind in (7, 8, 9):
+            remote(kind, j).start()
+
+    def forward(j):
+        remote(7, j).wait_recv()
+        remote(10, j).start()
+        remote(12, j).start()
+        remote(8, j).wait_recv()
+        remote(11, j).start()
+        remote(13, j).start()
+
+    def share(j):
+        remote(10, j).wait_recv()
+        remote(11, j).wait_recv()
+        remote(14, j).start()
+
+    def store(j):
+        return pltpu.make_async_copy(outb.at[j], out_ref.at[:, pl.ds(j * cb, cb)], stored.at[j])
+
+    def collect(j):
+        for kind in (9, 12, 13, 14):
+            remote(kind, j).wait_recv()
+        store(j).start()
+
+    stages = ((compute, 0), (chip_sum, 1), (combine, 3), (finish, 5), (forward, 7), (share, 9), (collect, 10))
+    for step in range(n_b + stages[-1][1]):
+        for stage, lag in stages:
+            if 0 <= step - lag < n_b:
+                stage(step - lag)
+    for j in range(n_b):
+        for kind in range(15):
+            remote(kind, j).wait_send()
+        store(j).wait()
+
+
+def mlp_and_sum(mesh, x, gamma, beta, context, w_out, w_up, w_down):
+    rows, width = x.shape
+    hidden = w_up.shape[1]
+    ctx_width = w_out.shape[0]
+    chips = mesh.shape['tp'] // 2
+    assert chips == 4
+    n_u, n_b = hidden // UP_COLS, width // OUT_COLS
+    half, slab = rows // 2, rows // 2 // chips
+
+    def block(dtype, *shape):
+        return pltpu.VMEM((n_b,) + shape, dtype)
+
+    return pl.pallas_call(
+        mlp_kernel,
+        out_shape=jax.ShapeDtypeStruct(x.shape, x.dtype),
+        in_specs=[VMEM, VMEM, VMEM, VMEM, ANY, ANY, ANY],
+        out_specs=ANY,
+        scratch_shapes=[
+            pltpu.VMEM((n_u, width, UP_COLS), BF16),
+            block(BF16, hidden, OUT_COLS),
+            block(BF16, ctx_width, OUT_COLS),
+            pltpu.VMEM((rows, width), BF16),
+            pltpu.VMEM((n_u, rows, UP_COLS), BF16),
+            pltpu.VMEM((rows, ctx_width), BF16),
+            block(F32, rows, OUT_COLS),
+            block(BF16, half, OUT_COLS),
+            block(BF16, half, OUT_COLS),
+            block(F32, half, OUT_COLS),
+            block(BF16, half, OUT_COLS),
+            block(BF16, slab, OUT_COLS // 2),
+            block(BF16, slab, OUT_COLS // 2),
+            block(BF16, slab, OUT_COLS // 2),
+            block(BF16, slab, OUT_COLS // 2),
+            block(BF16, slab, OUT_COLS),
+            block(BF16, slab, OUT_COLS),
+            block(BF16, rows, OUT_COLS),
+            pltpu.SemaphoreType.DMA((n_u,)),
+            pltpu.SemaphoreType.DMA((n_b,)),
+            pltpu.SemaphoreType.DMA((n_b,)),
+            pltpu.SemaphoreType.DMA((15, n_b)),
+            pltpu.SemaphoreType.DMA((15, n_b)),
+            pltpu.SemaphoreType.DMA((n_b,)),
+        ],
+        compiler_params=pltpu.CompilerParams(vmem_limit_bytes=60 * 1024 * 1024, collective_id=0, has_side_effects=True),
+        name='mlp_and_sum',
+    )(x, gamma.reshape(-1, LANES), beta.reshape(-1, LANES), context, w_out, w_up, w_down)
 
 
 def solution(mesh):
@@ -199,15 +386,8 @@
     cache_spec = P('dp', 'tp', None, None)
 
     def device_step(x, ln_attn_gamma, ln_attn_beta, ln_mlp_gamma, ln_mlp_beta, w_qkv, w_out, w_up, w_down, k_cache, v_cache, positions):
-        mlp_in = layer_norm(x, ln_mlp_gamma, ln_mlp_beta)
         context, keys_all, values_all = attend(x, ln_attn_gamma, ln_attn_beta, w_qkv, k_cache, v_cache, positions)
-        rows = x.shape[0]
-        context = context.astype(BF16).reshape(rows, -1)
-        attn_part = jnp.dot(context, w_out.reshape(-1, x.shape[1]), preferred_element_type=jnp.float32)
-        hidden = jax.nn.gelu(jnp.dot(mlp_in, w_up, preferred_element_type=jnp.float32), approximate=False).astype(jnp.bfloat16)
-        mlp_part = jnp.dot(hidden, w_down, preferred_element_type=jnp.float32)
-        total = lax.psum((attn_part + mlp_part).astype(BF16), 'tp')
-        layer_out = (x.astype(jnp.float32) + total.astype(jnp.float32)).astype(jnp.bfloat16)
+        layer_out = mlp_and_sum(mesh, x, ln_mlp_gamma, ln_mlp_beta, context, w_out.reshape(-1, x.shape[1]), w_up, w_down)
         return layer_out, keys_all, values_all
 
     return jax.shard_map(device_step, mesh=mesh, in_specs=(row_spec, vec_spec, vec_spec, vec_spec, vec_spec, P(None, 'tp', None, None), P('tp', None, None, None), P(None, 'tp'), P('tp', None), cache_spec, cache_spec, P('dp')), out_specs=(row_spec, cache_spec, cache_spec), check_vma=False)

time: 143 us -> 92.5 us (0.65); the launches traced: 141 us -> 92.3 us
  waiting for transfers between devices: 55.4 us -> 0 us
  Pallas kernels: 44.5 us -> 87.7 us
  matrix products: 18.3 us -> 0 us
  between operations: 14.1 us -> 0.65 us
  other arithmetic: 8.27 us -> 1.74 us
  local copies, waits for them, and re-layouts: 0.1 us -> 2.29 us
    psum x1 -> x0, waiting for transfers between devices: 55.3 us -> none  [device_step(): total = lax.psum((attn_part + mlp_part).astype(BF16), 'tp')]
    pallas_call x0 -> x1, Pallas kernels: none -> 43.3 us  [mlp_and_sum(): pl.pallas_call(mlp_kernel, out_shape=jax.ShapeDtypeStruct(x.shape, x.dtyp...]
    dot_general x2 -> x0, matrix products: 18.3 us -> none  [the longest x1 14.3 us: device_step(): mlp_part = jnp.dot(hidden, w_down, preferred_element_type=jnp.float32)]
    convert_element_type x2 -> x0, other arithmetic: 3.41 us -> none  [the longest x1 2.44 us: device_step(): (x.astype(jnp.float32) + total.astype(jnp.float32)).astype(jnp.bfloat16)]
    reduce_sum x2 -> x0, other arithmetic: 3.1 us -> none  [the longest x1 1.65 us: layer_norm(): row_var = jnp.mean(centred * centred, axis=-1, keepdims=True)]
    unnamed x6 -> x1, local copies, waits for them, and re-layouts: 0.01 us -> 2.29 us
  transfers between devices with their start and end apart: 1 -> 0, of which waited for: 1 -> 0; matrix products, arithmetic and copies ran while one was open for 0% -> 0% of each run, Pallas kernels for 0% -> 0%
where the time goes in v2:
time: 92.5 us; the launch traced here: 92.3 us
  Pallas kernels  87.7 us (95%)
  local copies, waits for them, and re-layouts  2.29 us (2%)
  other arithmetic  1.74 us (2%)
    pallas_call x1, Pallas kernels, attend(): pl.pallas_call(attention_kernel, out_shape=[jax.ShapeDtypeStruct((rows *...  44.4 us
    pallas_call x1, Pallas kernels, mlp_and_sum(): pl.pallas_call(mlp_kernel, out_shape=jax.ShapeDtypeStruct(x.shape, x.dtyp...  43.3 us
    unnamed x1, local copies, waits for them, and re-layouts  2.29 us

profile of v2, /device:TPU:113, one launch (start us, length us, event | category | flops | bytes accessed | tf_op | source)
XLA Modules:
  0.0 92.3 jit_solution(11121559092441036344)
XLA Ops:
  0.6 0.7 convert_element_type.3
  1.3 0.3 fusion
  1.6 0.8 pad_maximum_fusion
  2.4 44.4 %attend.1 = (f32[512,128]{1,0:T(8,128)}, bf16[128,4,128,128]{3,2,1,0:T(8,128)(2,1)}, bf16[128,4,128,128]{3,2,1,0:T(8,128)(2,1)}) custom-call(s32[128]{0:T(128)} %pos_ref.1, bf16[128,4096]{1,0:T(8,128)(2,1)} %x_ref.3, f32[32,128]{1,0:T(8,128)} %bitcast.10, f32[32,128]{1,0:T(8,128)} %bitcast.11, f32[128,128]{1,0:T(8,128)} %get-tuple-element.12.cos_ref, ...), custom_call_target="tpu_custom_call" | custom-call | tf_op jit(solution)/shard_map/attend/pallas_call | solution.py:163
  46.8 43.3 %mlp_and_sum.1 = bf16[128,4096]{1,0:T(8,128)(2,1)} custom-call(bf16[128,4096]{1,0:T(8,128)(2,1)} %x_ref.3, f32[32,128]{1,0:T(8,128)} %bitcast.12, f32[32,128]{1,0:T(8,128)} %bitcast.13, f32[512,128]{1,0:T(8,128)} %get-tuple-element.6.ctx_ref, bf16[512,4096]{1,0:T(8,128)(2,1)} %bitcast.9, bf16[4096,2048]{1,0:T(8,128)(2,1)} %wu_ref.1, bf16[2048,4096]{1,0:T(8,128)(2,1)} %wd_ref.1), custom_call_target="tpu_custom_call" | custom-call | tf_op jit(solution)/shard_map/mlp_and_sum/pallas_call | solution.py:347
  90.1 2.3 %copy.16 = bf16[128,4096]{1,0:T(8,128)(2,1)} copy(bf16[128,4096]{1,0:T(8,128)(2,1)} %mlp_and_sum.1) | data formatting | bytes 2097152
  (1 shorter events, 0.0 us)

commit v3 on v2

--- a/solution.py
+++ b/solution.py
@@ -101,8 +101,9 @@
         vn_s[at, :] = acc[:, (2 * groups + g) * head:(2 * groups + g + 1) * head].astype(BF16).astype(F32)
 
     row16 = lax.broadcasted_iota(jnp.int32, (16, head), 0)
-    row8 = lax.broadcasted_iota(jnp.int32, (2 * groups, slots), 0)
-    lane8 = lax.broadcasted_iota(jnp.int32, (2 * groups, slots), 1)
+    per_chunk = ROWS_PER_CHUNK * groups
+    slot_id = lax.broadcasted_iota(jnp.int32, (slots, per_chunk), 0)
+    lane_id = lax.broadcasted_iota(jnp.int32, (slots, per_chunk), 1)
     scale = head ** -0.5
 
     def chunk(i, carry):
@@ -125,22 +126,26 @@
         io(i, 0, True).start()
         io(i, 1, True).start()
 
-        for pair in range(ROWS_PER_CHUNK // 2):
-            b = i * ROWS_PER_CHUNK + 2 * pair
-            at = pl.ds(pl.multiple_of(b * groups, 2 * groups), 2 * groups)
-            q8 = q_s[at, :].astype(BF16)
-            keys = kbuf[pl.ds(b, 2)].reshape(2 * groups * slots, head)
-            every = lax.dot_general(q8, keys, (((1,), (1,)), ((), ())), preferred_element_type=F32)
-            s = every[:, 0:slots]
-            for t in range(1, 2 * groups):
-                s = jnp.where(row8 == t, every[:, t * slots:(t + 1) * slots], s)
-            pos8 = jnp.where(row8 < groups, pos_ref[b], pos_ref[b + 1])
-            s = jnp.where(lane8 <= pos8, s * scale, NEG_BIG)
-            e = jnp.exp(s - jnp.max(s, axis=-1, keepdims=True))
-            p = e / jnp.sum(e, axis=-1, keepdims=True)
-            spread = jnp.concatenate([jnp.where(row8 == t, p, 0.0) for t in range(2 * groups)], axis=1).astype(BF16)
-            values = vbuf[pl.ds(b, 2)].reshape(2 * groups * slots, head)
-            ctx_ref[at, :] = jnp.dot(spread, values, preferred_element_type=F32).astype(BF16).astype(F32)
+        at = pl.ds(pl.multiple_of(i * per_chunk, per_chunk), per_chunk)
+        queries = q_s[at, :].astype(BF16)
+        s = jnp.zeros((slots, per_chunk), F32)
+        limit = jnp.zeros((slots, per_chunk), jnp.int32)
+        for r in range(ROWS_PER_CHUNK):
+            b = i * ROWS_PER_CHUNK + r
+            every = lax.dot_general(kbuf[b].reshape(groups * slots, head), queries, (((1,), (1,)), ((), ())),
+                                    preferred_element_type=F32)
+            for g in range(groups):
+                s = jnp.where(lane_id == r * groups + g, every[g * slots:(g + 1) * slots], s)
+            limit = jnp.where(lane_id >= r * groups, pos_ref[b], limit)
+        s = jnp.where(slot_id <= limit, s * scale, NEG_BIG)
+        e = jnp.exp(s - jnp.max(s, axis=0, keepdims=True))
+        p = (e / jnp.sum(e, axis=0, keepdims=True)).astype(BF16).astype(F32)
+        for r in range(ROWS_PER_CHUNK):
+            b = i * ROWS_PER_CHUNK + r
+            for g in range(groups):
+                n = r * groups + g
+                weighted = jnp.broadcast_to(p[:, n:n + 1], (slots, head)) * vbuf[b, g].astype(F32)
+                ctx_ref[pl.ds(b * groups + g, 1), :] = jnp.sum(weighted, axis=0, keepdims=True).astype(BF16).astype(F32)
         return carry
 
     lax.fori_loop(0, n_c, chunk, 0)
@@ -187,14 +192,15 @@
 
 
 def mlp_kernel(x_ref, gamma_ref, beta_ref, ctx_ref, wo_ref, wu_ref, wd_ref, out_ref,
-               wub, wdb, wob, mlp_in, hid, ctxb, part, d2d_src, d2d_dst, cs32, csb, relay_a, relay_b, comb_a, comb_b,
+               wub, wcat, mlp_in, lhs, part, d2d_src, d2d_dst, cs32, csb, relay_a, relay_b, comb_a, comb_b,
                from_l, from_r, outb, usem, dsem, osem, send, recv, stored):
     n_u, _, cu = wub.shape
-    n_b, _, cb = wdb.shape
+    n_b, _, cb = wcat.shape
     half, slab = d2d_src.shape[1], relay_a.shape[1]
     chips = half // slab
-    groups = ctxb.shape[1] // LANES
     rows = x_ref.shape[0]
+    ctx_width = wo_ref.shape[0]
+    groups = ctx_width // LANES
     me = lax.axis_index('tp')
     p, c = lax.div(me, 2), lax.rem(me, 2)
     right = 2 * lax.rem(p + 1, chips) + c
@@ -206,10 +212,10 @@
         return pltpu.make_async_copy(wu_ref.at[:, pl.ds(u * cu, cu)], wub.at[u], usem.at[u])
 
     def down_copy(j):
-        return pltpu.make_async_copy(wd_ref.at[:, pl.ds(j * cb, cb)], wdb.at[j], dsem.at[j])
+        return pltpu.make_async_copy(wd_ref.at[:, pl.ds(j * cb, cb)], wcat.at[j, pl.ds(ctx_width, wd_ref.shape[0])], dsem.at[j])
 
     def out_copy(j):
-        return pltpu.make_async_copy(wo_ref.at[:, pl.ds(j * cb, cb)], wob.at[j], osem.at[j])
+        return pltpu.make_async_copy(wo_ref.at[:, pl.ds(j * cb, cb)], wcat.at[j, pl.ds(0, ctx_width)], osem.at[j])
 
     for u in range(n_u):
         up_copy(u).start()
@@ -251,12 +257,12 @@
 
     norm_into(x_ref, gamma_ref, beta_ref, mlp_in)
     for g in range(groups):
-        ctxb[:, g * LANES:(g + 1) * LANES] = ctx_ref[pl.ds(g, rows, stride=groups), :].astype(BF16)
+        lhs[:, g * LANES:(g + 1) * LANES] = ctx_ref[pl.ds(g, rows, stride=groups), :].astype(BF16)
 
     def up(u, carry):
         up_copy(u).wait()
         z = jnp.dot(mlp_in[...], wub[u], preferred_element_type=F32)
-        hid[u] = (0.5 * z * (1.0 + lax.erf(z * 0.5 ** 0.5))).astype(BF16)
+        lhs[:, pl.ds(pl.multiple_of(ctx_width + u * cu, cu), cu)] = (0.5 * z * (1.0 + lax.erf(z * 0.5 ** 0.5))).astype(BF16)
         return carry
 
     lax.fori_loop(0, n_u, up, 0)
@@ -267,11 +273,8 @@
 
     def compute(j):
         out_copy(j).wait()
-        y = jnp.dot(ctxb[...], wob[j], preferred_element_type=F32)
         down_copy(j).wait()
-        for u in range(n_u):
-            y += jnp.dot(hid[u], wdb[j, u * cu:(u + 1) * cu, :], preferred_element_type=F32)
-        part[j] = y
+        part[j] = jnp.dot(lhs[...], wcat[j], preferred_element_type=F32)
         d2d_src[j] = part[j, other_half].astype(BF16)
         remote(0, j).start()
 
@@ -351,11 +354,9 @@
         out_specs=ANY,
         scratch_shapes=[
             pltpu.VMEM((n_u, width, UP_COLS), BF16),
-            block(BF16, hidden, OUT_COLS),
-            block(BF16, ctx_width, OUT_COLS),
+            block(BF16, ctx_width + hidden, OUT_COLS),
             pltpu.VMEM((rows, width), BF16),
-            pltpu.VMEM((n_u, rows, UP_COLS), BF16),
-            pltpu.VMEM((rows, ctx_width), BF16),
+            pltpu.VMEM((rows, ctx_width + hidden), BF16),
             block(F32, rows, OUT_COLS),
             block(BF16, half, OUT_COLS),
             block(BF16, half, OUT_COLS),

time: 92.5 us -> 81.2 us (0.88)
  Pallas kernels: 87.7 us -> 76.4 us
    pallas_call x1, Pallas kernels: 44.4 us -> 33 us  [attend(): pl.pallas_call(attention_kernel, out_shape=[jax.ShapeDtypeStruct((rows *...]
where the time goes in v3:
time: 81.2 us; the launch traced here: 81.1 us
  Pallas kernels  76.4 us (94%)
  local copies, waits for them, and re-layouts  2.29 us (3%)
  other arithmetic  1.74 us (2%)
    pallas_call x1, Pallas kernels, mlp_and_sum(): pl.pallas_call(mlp_kernel, out_shape=jax.ShapeDtypeStruct(x.shape, x.dtyp...  43.4 us
    pallas_call x1, Pallas kernels, attend(): pl.pallas_call(attention_kernel, out_shape=[jax.ShapeDtypeStruct((rows *...  33 us
    unnamed x1, local copies, waits for them, and re-layouts  2.29 us

profile of v3, /device:TPU:113, one launch (start us, length us, event | category | flops | bytes accessed | tf_op | source)
XLA Modules:
  0.0 81.1 jit_solution(12257318696747249247)
XLA Ops:
  0.6 0.7 convert_element_type.3
  1.3 0.3 fusion
  1.6 0.8 pad_maximum_fusion
  2.4 33.0 %attend.1 = (f32[512,128]{1,0:T(8,128)}, bf16[128,4,128,128]{3,2,1,0:T(8,128)(2,1)}, bf16[128,4,128,128]{3,2,1,0:T(8,128)(2,1)}) custom-call(s32[128]{0:T(128)} %pos_ref.1, bf16[128,4096]{1,0:T(8,128)(2,1)} %x_ref.3, f32[32,128]{1,0:T(8,128)} %bitcast.10, f32[32,128]{1,0:T(8,128)} %bitcast.11, f32[128,128]{1,0:T(8,128)} %get-tuple-element.12.cos_ref, ...), custom_call_target="tpu_custom_call" | custom-call | tf_op jit(solution)/shard_map/attend/pallas_call | solution.py:168
  35.4 43.4 %mlp_and_sum.1 = bf16[128,4096]{1,0:T(8,128)(2,1)} custom-call(bf16[128,4096]{1,0:T(8,128)(2,1)} %x_ref.3, f32[32,128]{1,0:T(8,128)} %bitcast.12, f32[32,128]{1,0:T(8,128)} %bitcast.13, f32[512,128]{1,0:T(8,128)} %get-tuple-element.6.ctx_ref, bf16[512,4096]{1,0:T(8,128)(2,1)} %bitcast.9, bf16[4096,2048]{1,0:T(8,128)(2,1)} %wu_ref.1, bf16[2048,4096]{1,0:T(8,128)(2,1)} %wd_ref.1), custom_call_target="tpu_custom_call" | custom-call | tf_op jit(solution)/shard_map/mlp_and_sum/pallas_call | solution.py:350
  78.8 2.3 %copy.16 = bf16[128,4096]{1,0:T(8,128)(2,1)} copy(bf16[128,4096]{1,0:T(8,128)(2,1)} %mlp_and_sum.1) | data formatting | bytes 2097152
  (1 shorter events, 0.0 us)

commit v4 on v3

--- a/solution.py
+++ b/solution.py
@@ -1,3 +1,5 @@
+import math
+
 import jax
 import jax.numpy as jnp
 from jax import lax
@@ -11,13 +13,15 @@
 LANES = 128
 ROWS_PER_CHUNK = 8
 W_CHUNK = 256
-UP_COLS = 512
+W_AHEAD = 8
+KV_AHEAD = 6
+UP_COLS = 256
+AHEAD = 4
 OUT_COLS = 512
+BLOCK_US = 0.9
 F32 = jnp.float32
 BF16 = jnp.bfloat16
-ANY = pl.BlockSpec(memory_space=pl.ANY)
-VMEM = pl.BlockSpec(memory_space=pltpu.VMEM)
-SMEM = pl.BlockSpec(memory_space=pltpu.SMEM)
+HBM = pl.BlockSpec(memory_space=pltpu.HBM)
 MESH = pl.DeviceIdType.MESH
 
 
@@ -47,8 +51,9 @@
     lax.fori_loop(0, tiles, write, 0, unroll=4)
 
 
-def attention_kernel(pos_ref, x_ref, gamma_ref, beta_ref, cos_ref, sin_ref, w_ref, k_ref, v_ref, ctx_ref, ko_ref, vo_ref,
-                     wbuf, wf, acc, attn, q_s, kn_s, vn_s, kbuf, vbuf, wsem, insem, outsem):
+def attention_kernel(pos_hbm, pos_row_hbm, x_hbm, gamma_hbm, beta_hbm, w_ref, k_ref, v_ref, ctx_hbm, ko_ref, vo_ref,
+                     pos_ref, pos_row, x_ref, gamma_ref, beta_ref, ctx_ref,
+                     wbuf, wf, acc, attn, q_s, kn_s, vn_s, kbuf, vbuf, small, wsem, insem, outsem):
     rows, width = x_ref.shape
     _, groups, slots, head = k_ref.shape
     cols = 3 * groups
@@ -67,17 +72,33 @@
             return pltpu.make_async_copy(buf.at[at], hbm_out.at[at], outsem.at[which, i])
         return pltpu.make_async_copy(hbm_in.at[at], buf.at[at], insem.at[which, i])
 
-    for c in range(n_w):
-        w_copy(c).start()
-    for i in range(n_c):
+    def kv_start(i):
         io(i, 0, False).start()
         io(i, 1, False).start()
 
+    first = [pltpu.make_async_copy(src, dst, small.at[n]) for n, (src, dst) in enumerate(
+        ((x_hbm, x_ref), (gamma_hbm, gamma_ref), (beta_hbm, beta_ref), (pos_row_hbm, pos_row), (pos_hbm, pos_ref)))]
+    for copy in first:
+        copy.start()
+    for c in range(W_AHEAD):
+        w_copy(c).start()
+    for copy in first:
+        copy.wait()
+
     norm_into(x_ref, gamma_ref, beta_ref, attn)
     acc[...] = jnp.zeros_like(acc)
 
     def project(c, carry):
         w_copy(c).wait()
+
+        @pl.when(c + W_AHEAD < n_w)
+        def _():
+            w_copy(c + W_AHEAD).start()
+
+        @pl.when(c >= n_w - KV_AHEAD)
+        def _():
+            kv_start(c - (n_w - KV_AHEAD))
+
         wf[...] = wbuf[pl.ds(pl.multiple_of(c * wrows, wrows), wrows), :].astype(F32)
         lhs = attn[:, pl.ds(pl.multiple_of(c * W_CHUNK, W_CHUNK), W_CHUNK)]
         for n in range(0, cols, 2):
@@ -88,7 +109,11 @@
 
     lax.fori_loop(0, n_w, project, 0)
 
-    cos_t, sin_t = cos_ref[...], sin_ref[...]
+    lane = lax.broadcasted_iota(jnp.int32, (rows, head), 1)
+    freq = jnp.exp(lax.rem(lane, head // 2).astype(F32) * (-2.0 * math.log(ROPE_BASE) / head))
+    angle = jnp.broadcast_to(pos_row[...].astype(F32), (rows, rows)).T * freq
+    cos_t = jnp.cos(angle)
+    sin_t = jnp.where(lane < head // 2, -1.0, 1.0) * jnp.sin(angle)
 
     def rotate(u):
         u = u.astype(BF16).astype(F32)
@@ -109,6 +134,10 @@
     def chunk(i, carry):
         io(i, 0, False).wait()
         io(i, 1, False).wait()
+
+        @pl.when(i + KV_AHEAD < n_c)
+        def _():
+            kv_start(i + KV_AHEAD)
 
         def write_row(r, carry):
             b = i * ROWS_PER_CHUNK + r
@@ -149,20 +178,18 @@
         return carry
 
     lax.fori_loop(0, n_c, chunk, 0)
+    ctx_out = pltpu.make_async_copy(ctx_ref, ctx_hbm, small.at[0])
+    ctx_out.start()
     for i in range(n_c):
         io(i, 0, True).wait()
         io(i, 1, True).wait()
+    ctx_out.wait()
 
 
 def attend(x, gamma, beta, w_qkv, k_cache, v_cache, positions):
     rows, width = x.shape
     _, groups, slots, head = k_cache.shape
     cols = 3 * groups
-    inv_freq = ROPE_BASE ** (-2.0 * jnp.arange(head // 2, dtype=F32) / head)
-    angles = positions.astype(F32)[:, None] * inv_freq[None, :]
-    cos_t, sin_t = jnp.cos(angles), jnp.sin(angles)
-    cos_t = jnp.concatenate([cos_t, cos_t], axis=1)
-    sin_t = jnp.concatenate([-sin_t, sin_t], axis=1)
     w_rows = jnp.transpose(w_qkv, (0, 2, 1, 3)).reshape(width * cols, head)
     n_w, n_c = width // W_CHUNK, rows // ROWS_PER_CHUNK
     return pl.pallas_call(
@@ -170,9 +197,15 @@
         out_shape=[jax.ShapeDtypeStruct((rows * groups, head), F32),
                    jax.ShapeDtypeStruct(k_cache.shape, k_cache.dtype),
                    jax.ShapeDtypeStruct(v_cache.shape, v_cache.dtype)],
-        in_specs=[SMEM, VMEM, VMEM, VMEM, VMEM, VMEM, ANY, ANY, ANY],
-        out_specs=[VMEM, ANY, ANY],
+        in_specs=[HBM] * 8,
+        out_specs=[HBM] * 3,
         scratch_shapes=[
+            pltpu.SMEM((rows,), jnp.int32),
+            pltpu.VMEM((1, rows), jnp.int32),
+            pltpu.VMEM((rows, width), BF16),
+            pltpu.VMEM((width // LANES, LANES), F32),
+            pltpu.VMEM((width // LANES, LANES), F32),
+            pltpu.VMEM((rows * groups, head), F32),
             pltpu.VMEM((width * cols, head), BF16),
             pltpu.VMEM((W_CHUNK * cols, head), F32),
             pltpu.VMEM((rows, cols * head), F32),
@@ -182,17 +215,18 @@
             pltpu.VMEM((rows * groups, head), F32),
             pltpu.VMEM(k_cache.shape, BF16),
             pltpu.VMEM(v_cache.shape, BF16),
+            pltpu.SemaphoreType.DMA((5,)),
             pltpu.SemaphoreType.DMA((n_w,)),
             pltpu.SemaphoreType.DMA((2, n_c)),
             pltpu.SemaphoreType.DMA((2, n_c)),
         ],
         compiler_params=pltpu.CompilerParams(vmem_limit_bytes=60 * 1024 * 1024),
         name='attend',
-    )(positions, x, gamma.reshape(-1, LANES), beta.reshape(-1, LANES), cos_t, sin_t, w_rows, k_cache, v_cache)
-
-
-def mlp_kernel(x_ref, gamma_ref, beta_ref, ctx_ref, wo_ref, wu_ref, wd_ref, out_ref,
-               wub, wcat, mlp_in, lhs, part, d2d_src, d2d_dst, cs32, csb, relay_a, relay_b, comb_a, comb_b,
+    )(positions, positions.reshape(1, rows), x, gamma.reshape(-1, LANES), beta.reshape(-1, LANES), w_rows, k_cache, v_cache)
+
+
+def mlp_kernel(x_hbm, gamma_hbm, beta_hbm, ctx_hbm, wo_ref, wu_ref, wd_ref, out_ref,
+               x_ref, gamma_ref, beta_ref, ctx_ref, small, wub, wcat, mlp_in, lhs, part, d2d_src, d2d_dst, cs32, csb, relay_a, relay_b, comb_a, comb_b,
                from_l, from_r, outb, usem, dsem, osem, send, recv, stored):
     n_u, _, cu = wub.shape
     n_b, _, cb = wcat.shape
@@ -217,11 +251,19 @@
     def out_copy(j):
         return pltpu.make_async_copy(wo_ref.at[:, pl.ds(j * cb, cb)], wcat.at[j, pl.ds(0, ctx_width)], osem.at[j])
 
-    for u in range(n_u):
-        up_copy(u).start()
-    for j in range(n_b):
-        out_copy(j).start()
-        down_copy(j).start()
+    def fetch(n):
+        if n < n_u:
+            up_copy(n).start()
+        elif n < n_u + n_b:
+            out_copy(n - n_u).start()
+            down_copy(n - n_u).start()
+
+    first = [pltpu.make_async_copy(src, dst, small.at[n]) for n, (src, dst) in enumerate(
+        ((x_hbm, x_ref), (gamma_hbm, gamma_ref), (beta_hbm, beta_ref), (ctx_hbm, ctx_ref)))]
+    for copy in first:
+        copy.start()
+    for n in range(AHEAD):
+        fetch(n)
 
     barrier = pltpu.get_barrier_semaphore()
     for peer in (right, left, partner):
@@ -255,17 +297,19 @@
         return pltpu.make_async_remote_copy(src_ref=src, dst_ref=dst, send_sem=send.at[kind, j], recv_sem=recv.at[kind, j],
                                             device_id={'tp': peer}, device_id_type=MESH)
 
+    for copy in first:
+        copy.wait()
     norm_into(x_ref, gamma_ref, beta_ref, mlp_in)
     for g in range(groups):
         lhs[:, g * LANES:(g + 1) * LANES] = ctx_ref[pl.ds(g, rows, stride=groups), :].astype(BF16)
 
-    def up(u, carry):
+    for u in range(n_u):
         up_copy(u).wait()
+        fetch(u + AHEAD)
         z = jnp.dot(mlp_in[...], wub[u], preferred_element_type=F32)
-        lhs[:, pl.ds(pl.multiple_of(ctx_width + u * cu, cu), cu)] = (0.5 * z * (1.0 + lax.erf(z * 0.5 ** 0.5))).astype(BF16)
-        return carry
-
-    lax.fori_loop(0, n_u, up, 0)
+        at = ctx_width + u * cu
+        lhs[:, at:at + cu] = (0.5 * z * (1.0 + lax.erf(z * 0.5 ** 0.5))).astype(BF16)
+
     pl.semaphore_wait(barrier, 3)
 
     own_half = pl.ds(pl.multiple_of(c * half, half), half)
@@ -274,6 +318,7 @@
     def compute(j):
         out_copy(j).wait()
         down_copy(j).wait()
+        fetch(n_u + j + AHEAD)
         part[j] = jnp.dot(lhs[...], wcat[j], preferred_element_type=F32)
         d2d_src[j] = part[j, other_half].astype(BF16)
         remote(0, j).start()
@@ -324,11 +369,10 @@
             remote(kind, j).wait_recv()
         store(j).start()
 
-    stages = ((compute, 0), (chip_sum, 1), (combine, 3), (finish, 5), (forward, 7), (share, 9), (collect, 10))
-    for step in range(n_b + stages[-1][1]):
-        for stage, lag in stages:
-            if 0 <= step - lag < n_b:
-                stage(step - lag)
+    stages = ((compute, 0.0), (chip_sum, 1.4), (combine, 3.8), (finish, 6.2), (forward, 8.6), (share, 11.0), (collect, 12.4))
+    plan = sorted((j * BLOCK_US + after, n, j) for n, (_, after) in enumerate(stages) for j in range(n_b))
+    for _, n, j in plan:
+        stages[n][0](j)
     for j in range(n_b):
         for kind in range(15):
             remote(kind, j).wait_send()
@@ -350,9 +394,14 @@
     return pl.pallas_call(
         mlp_kernel,
         out_shape=jax.ShapeDtypeStruct(x.shape, x.dtype),
-        in_specs=[VMEM, VMEM, VMEM, VMEM, ANY, ANY, ANY],
-        out_specs=ANY,
+        in_specs=[HBM] * 7,
+        out_specs=HBM,
         scratch_shapes=[
+            pltpu.VMEM((rows, width), BF16),
+            pltpu.VMEM((width // LANES, LANES), F32),
+            pltpu.VMEM((width // LANES, LANES), F32),
+            pltpu.VMEM(context.shape, F32),
+            pltpu.SemaphoreType.DMA((4,)),
             pltpu.VMEM((n_u, width, UP_COLS), BF16),
             block(BF16, ctx_width + hidden, OUT_COLS),
             pltpu.VMEM((rows, width), BF16),

time: 81.2 us -> 73.1 us (0.900)
  Pallas kernels: 76.4 us -> 70 us
  other arithmetic: 1.74 us -> 0 us
    pallas_call x1, Pallas kernels: 43.4 us -> 38.5 us  [mlp_and_sum(): pl.pallas_call(mlp_kernel, out_shape=jax.ShapeDtypeStruct(x.shape, x.dtyp...]
    pallas_call x1, Pallas kernels: 33 us -> 31.5 us  [attend(): pl.pallas_call(attention_kernel, out_shape=[jax.ShapeDtypeStruct((rows *...]
where the time goes in v4:
time: 73.1 us; the launch traced here: 73 us
  Pallas kernels  70 us (96%)
  local copies, waits for them, and re-layouts  2.29 us (3%)
    pallas_call x1, Pallas kernels, mlp_and_sum(): pl.pallas_call(mlp_kernel, out_shape=jax.ShapeDtypeStruct(x.shape, x.dtyp...  38.5 us
    pallas_call x1, Pallas kernels, attend(): pl.pallas_call(attention_kernel, out_shape=[jax.ShapeDtypeStruct((rows *...  31.5 us
    unnamed x1, local copies, waits for them, and re-layouts  2.29 us

profile of v4, /device:TPU:113, one launch (start us, length us, event | category | flops | bytes accessed | tf_op | source)
XLA Modules:
  0.0 73.0 jit_solution(11993822617980818796)
XLA Ops:
  0.6 31.5 %attend.1 = (f32[512,128]{1,0:T(8,128)}, bf16[128,4,128,128]{3,2,1,0:T(8,128)(2,1)}, bf16[128,4,128,128]{3,2,1,0:T(8,128)(2,1)}) custom-call(s32[128]{0:T(128)} %pos_hbm.1, s32[1,128]{1,0:T(1,128)} %bitcast.15, bf16[128,4096]{1,0:T(8,128)(2,1)} %x_hbm.3, f32[32,128]{1,0:T(8,128)} %bitcast.11, f32[32,128]{1,0:T(8,128)} %bitcast.12, ...), custom_call_target="tpu_custom_call" | custom-call | tf_op jit(solution)/shard_map/attend/pallas_call | solution.py:195
  32.2 38.5 %mlp_and_sum.1 = bf16[128,4096]{1,0:T(8,128)(2,1)} custom-call(bf16[128,4096]{1,0:T(8,128)(2,1)} %x_hbm.3, f32[32,128]{1,0:T(8,128)} %bitcast.13, f32[32,128]{1,0:T(8,128)} %bitcast.14, f32[512,128]{1,0:T(8,128)} %get-tuple-element.6.ctx_hbm, bf16[512,4096]{1,0:T(8,128)(2,1)} %bitcast.10, bf16[4096,2048]{1,0:T(8,128)(2,1)} %wu_ref.1, bf16[2048,4096]{1,0:T(8,128)(2,1)} %wd_ref.1), custom_call_target="tpu_custom_call" | custom-call | tf_op jit(solution)/shard_map/mlp_and_sum/pallas_call | solution.py:394
  70.7 2.3 %copy.16 = bf16[128,4096]{1,0:T(8,128)(2,1)} copy(bf16[128,4096]{1,0:T(8,128)(2,1)} %mlp_and_sum.1) | data formatting | bytes 2097152

commit v5 on v4

--- a/solution.py
+++ b/solution.py
@@ -16,7 +16,7 @@
 W_AHEAD = 8
 KV_AHEAD = 6
 UP_COLS = 256
-AHEAD = 4
+AHEAD = 2
 OUT_COLS = 512
 BLOCK_US = 0.9
 F32 = jnp.float32
@@ -73,15 +73,15 @@
         return pltpu.make_async_copy(hbm_in.at[at], buf.at[at], insem.at[which, i])
 
     def kv_start(i):
-        io(i, 0, False).start()
-        io(i, 1, False).start()
+        io(i, 0, False).start(priority=1)
+        io(i, 1, False).start(priority=1)
 
     first = [pltpu.make_async_copy(src, dst, small.at[n]) for n, (src, dst) in enumerate(
         ((x_hbm, x_ref), (gamma_hbm, gamma_ref), (beta_hbm, beta_ref), (pos_row_hbm, pos_row), (pos_hbm, pos_ref)))]
     for copy in first:
         copy.start()
     for c in range(W_AHEAD):
-        w_copy(c).start()
+        w_copy(c).start(priority=1)
     for copy in first:
         copy.wait()
 
@@ -93,7 +93,7 @@
 
         @pl.when(c + W_AHEAD < n_w)
         def _():
-            w_copy(c + W_AHEAD).start()
+            w_copy(c + W_AHEAD).start(priority=1)
 
         @pl.when(c >= n_w - KV_AHEAD)
         def _():

time: 73.1 us -> 73 us (level)
    pallas_call x1, Pallas kernels: 31.5 us -> 30.5 us  [attend(): pl.pallas_call(attention_kernel, out_shape=[jax.ShapeDtypeStruct((rows *...]
    pallas_call x1, Pallas kernels: 38.5 us -> 39.4 us  [mlp_and_sum(): pl.pallas_call(mlp_kernel, out_shape=jax.ShapeDtypeStruct(x.shape, x.dtyp...]
where the time goes in v5:
time: 73 us; the launch traced here: 72.8 us
  Pallas kernels  69.9 us (96%)
  local copies, waits for them, and re-layouts  2.29 us (3%)
    pallas_call x1, Pallas kernels, mlp_and_sum(): pl.pallas_call(mlp_kernel, out_shape=jax.ShapeDtypeStruct(x.shape, x.dtyp...  39.4 us
    pallas_call x1, Pallas kernels, attend(): pl.pallas_call(attention_kernel, out_shape=[jax.ShapeDtypeStruct((rows *...  30.5 us
    unnamed x1, local copies, waits for them, and re-layouts  2.29 us

profile of v5, /device:TPU:113, one launch (start us, length us, event | category | flops | bytes accessed | tf_op | source)
XLA Modules:
  0.0 72.8 jit_solution(11877488116344807751)
XLA Ops:
  0.6 30.5 %attend.1 = (f32[512,128]{1,0:T(8,128)}, bf16[128,4,128,128]{3,2,1,0:T(8,128)(2,1)}, bf16[128,4,128,128]{3,2,1,0:T(8,128)(2,1)}) custom-call(s32[128]{0:T(128)} %pos_hbm.1, s32[1,128]{1,0:T(1,128)} %bitcast.15, bf16[128,4096]{1,0:T(8,128)(2,1)} %x_hbm.3, f32[32,128]{1,0:T(8,128)} %bitcast.11, f32[32,128]{1,0:T(8,128)} %bitcast.12, ...), custom_call_target="tpu_custom_call" | custom-call | tf_op jit(solution)/shard_map/attend/pallas_call | solution.py:195
  31.1 39.4 %mlp_and_sum.1 = bf16[128,4096]{1,0:T(8,128)(2,1)} custom-call(bf16[128,4096]{1,0:T(8,128)(2,1)} %x_hbm.3, f32[32,128]{1,0:T(8,128)} %bitcast.13, f32[32,128]{1,0:T(8,128)} %bitcast.14, f32[512,128]{1,0:T(8,128)} %get-tuple-element.6.ctx_hbm, bf16[512,4096]{1,0:T(8,128)(2,1)} %bitcast.10, bf16[4096,2048]{1,0:T(8,128)(2,1)} %wu_ref.1, bf16[2048,4096]{1,0:T(8,128)(2,1)} %wd_ref.1), custom_call_target="tpu_custom_call" | custom-call | tf_op jit(solution)/shard_map/mlp_and_sum/pallas_call | solution.py:394
  70.5 2.3 %copy.16 = bf16[128,4096]{1,0:T(8,128)(2,1)} copy(bf16[128,4096]{1,0:T(8,128)(2,1)} %mlp_and_sum.1) | data formatting | bytes 2097152

commit v6 on v5

--- a/solution.py
+++ b/solution.py
@@ -226,21 +226,21 @@
 
 
 def mlp_kernel(x_hbm, gamma_hbm, beta_hbm, ctx_hbm, wo_ref, wu_ref, wd_ref, out_ref,
-               x_ref, gamma_ref, beta_ref, ctx_ref, small, wub, wcat, mlp_in, lhs, part, d2d_src, d2d_dst, cs32, csb, relay_a, relay_b, comb_a, comb_b,
-               from_l, from_r, outb, usem, dsem, osem, send, recv, stored):
+               x_ref, gamma_ref, beta_ref, ctx_ref, small, wub, wcat, mlp_in, lhs, part, d2d_src, d2d_dst, cs32, csb, inbox, outb, usem, dsem, osem, send, recv, stored):
     n_u, _, cu = wub.shape
     n_b, _, cb = wcat.shape
-    half, slab = d2d_src.shape[1], relay_a.shape[1]
+    half, slab = d2d_src.shape[1], inbox.shape[2]
     chips = half // slab
     rows = x_ref.shape[0]
     ctx_width = wo_ref.shape[0]
     groups = ctx_width // LANES
     me = lax.axis_index('tp')
     p, c = lax.div(me, 2), lax.rem(me, 2)
-    right = 2 * lax.rem(p + 1, chips) + c
-    left = 2 * lax.rem(p + chips - 1, chips) + c
+    others = (2, 1, 3)
     partner = me + 1 - 2 * c
-    lo, hi = pl.ds(0, cb // 2), pl.ds(cb // 2, cb // 2)
+
+    def same_core(q):
+        return 2 * lax.rem(p + q, chips) + c
 
     def up_copy(u):
         return pltpu.make_async_copy(wu_ref.at[:, pl.ds(u * cu, cu)], wub.at[u], usem.at[u])
@@ -266,7 +266,7 @@
         fetch(n)
 
     barrier = pltpu.get_barrier_semaphore()
-    for peer in (right, left, partner):
+    for peer in tuple(same_core(q) for q in others) + (partner,):
         pl.semaphore_signal(barrier, inc=1, device_id={'tp': peer}, device_id_type=MESH)
 
     def in_half(q):
@@ -276,24 +276,19 @@
         return pl.ds(pl.multiple_of(core * half + lax.rem(p + q, chips) * slab, slab), slab)
 
     def remote(kind, j):
-        mine, before, after, far = (in_rows(q, c) for q in (0, chips - 1, 1, 2))
-        src, dst, peer = (
-            (d2d_src.at[j], d2d_dst.at[j], partner),
-            (csb.at[j, in_half(2), lo], relay_a.at[j], right),
-            (csb.at[j, in_half(2), hi], relay_b.at[j], left),
-            (csb.at[j, in_half(1), hi], from_l.at[j, :, hi], right),
-            (csb.at[j, in_half(chips - 1), lo], from_r.at[j, :, lo], left),
-            (comb_a.at[j], from_l.at[j, :, lo], right),
-            (comb_b.at[j], from_r.at[j, :, hi], left),
-            (outb.at[j, mine], outb.at[j, mine], right),
-            (outb.at[j, mine], outb.at[j, mine], left),
-            (outb.at[j, mine], outb.at[j, mine], partner),
-            (outb.at[j, before, lo], outb.at[j, before, lo], right),
-            (outb.at[j, after, hi], outb.at[j, after, hi], left),
-            (outb.at[j, before], outb.at[j, before], partner),
-            (outb.at[j, after], outb.at[j, after], partner),
-            (outb.at[j, far], outb.at[j, far], partner),
-        )[kind]
+        mine = in_rows(0, c)
+        if kind == 0:
+            src, dst, peer = d2d_src.at[j], d2d_dst.at[j], partner
+        elif kind < 4:
+            q = others[kind - 1]
+            src, dst, peer = csb.at[j, in_half(q)], inbox.at[j, kind - 1], same_core(q)
+        elif kind < 7:
+            src, dst, peer = outb.at[j, mine], outb.at[j, mine], same_core(others[kind - 4])
+        elif kind == 7:
+            src, dst, peer = outb.at[j, mine], outb.at[j, mine], partner
+        else:
+            far = in_rows(chips - others[kind - 8], c)
+            src, dst, peer = outb.at[j, far], outb.at[j, far], partner
         return pltpu.make_async_remote_copy(src_ref=src, dst_ref=dst, send_sem=send.at[kind, j], recv_sem=recv.at[kind, j],
                                             device_id={'tp': peer}, device_id_type=MESH)
 
@@ -310,7 +305,7 @@
         at = ctx_width + u * cu
         lhs[:, at:at + cu] = (0.5 * z * (1.0 + lax.erf(z * 0.5 ** 0.5))).astype(BF16)
 
-    pl.semaphore_wait(barrier, 3)
+    pl.semaphore_wait(barrier, 4)
 
     own_half = pl.ds(pl.multiple_of(c * half, half), half)
     other_half = pl.ds(pl.multiple_of((1 - c) * half, half), half)
@@ -328,53 +323,38 @@
         y = part[j, own_half] + d2d_dst[j].astype(F32)
         cs32[j] = y
         csb[j] = y.astype(BF16)
-        for kind in (1, 2, 3, 4):
+        for kind in (1, 2, 3):
             remote(kind, j).start()
 
-    def combine(j):
-        remote(1, j).wait_recv()
-        comb_a[j] = (cs32[j, in_half(1), lo] + relay_a[j].astype(F32)).astype(BF16)
-        remote(5, j).start()
-        remote(2, j).wait_recv()
-        comb_b[j] = (cs32[j, in_half(chips - 1), hi] + relay_b[j].astype(F32)).astype(BF16)
-        remote(6, j).start()
-
     def finish(j):
-        for kind in (3, 4, 5, 6):
+        y = cs32[j, in_half(0)]
+        for kind in (1, 2, 3):
             remote(kind, j).wait_recv()
+            y += inbox[j, kind - 1].astype(F32)
         mine = in_rows(0, c)
-        y = cs32[j, in_half(0)] + from_l[j].astype(F32) + from_r[j].astype(F32)
         outb[j, mine] = (x_ref[mine, j * cb:(j + 1) * cb].astype(F32) + y).astype(BF16)
-        for kind in (7, 8, 9):
+        for kind in (4, 5, 6, 7):
             remote(kind, j).start()
 
-    def forward(j):
-        remote(7, j).wait_recv()
-        remote(10, j).start()
-        remote(12, j).start()
-        remote(8, j).wait_recv()
-        remote(11, j).start()
-        remote(13, j).start()
-
     def share(j):
-        remote(10, j).wait_recv()
-        remote(11, j).wait_recv()
-        remote(14, j).start()
+        for kind in (4, 5, 6):
+            remote(kind, j).wait_recv()
+            remote(kind + 4, j).start()
 
     def store(j):
         return pltpu.make_async_copy(outb.at[j], out_ref.at[:, pl.ds(j * cb, cb)], stored.at[j])
 
     def collect(j):
-        for kind in (9, 12, 13, 14):
+        for kind in (7, 8, 9, 10):
             remote(kind, j).wait_recv()
         store(j).start()
 
-    stages = ((compute, 0.0), (chip_sum, 1.4), (combine, 3.8), (finish, 6.2), (forward, 8.6), (share, 11.0), (collect, 12.4))
+    stages = ((compute, 0.0), (chip_sum, 1.4), (finish, 5.0), (share, 8.6), (collect, 10.0))
     plan = sorted((j * BLOCK_US + after, n, j) for n, (_, after) in enumerate(stages) for j in range(n_b))
     for _, n, j in plan:
         stages[n][0](j)
     for j in range(n_b):
-        for kind in range(15):
+        for kind in range(11):
             remote(kind, j).wait_send()
         store(j).wait()
 
@@ -411,18 +391,13 @@
             block(BF16, half, OUT_COLS),
             block(F32, half, OUT_COLS),
             block(BF16, half, OUT_COLS),
-            block(BF16, slab, OUT_COLS // 2),
-            block(BF16, slab, OUT_COLS // 2),
-            block(BF16, slab, OUT_COLS // 2),
-            block(BF16, slab, OUT_COLS // 2),
-            block(BF16, slab, OUT_COLS),
-            block(BF16, slab, OUT_COLS),
+            block(BF16, chips - 1, slab, OUT_COLS),
             block(BF16, rows, OUT_COLS),
             pltpu.SemaphoreType.DMA((n_u,)),
             pltpu.SemaphoreType.DMA((n_b,)),
             pltpu.SemaphoreType.DMA((n_b,)),
-            pltpu.SemaphoreType.DMA((15, n_b)),
-            pltpu.SemaphoreType.DMA((15, n_b)),
+            pltpu.SemaphoreType.DMA((11, n_b)),
+            pltpu.SemaphoreType.DMA((11, n_b)),
             pltpu.SemaphoreType.DMA((n_b,)),
         ],
         compiler_params=pltpu.CompilerParams(vmem_limit_bytes=60 * 1024 * 1024, collective_id=0, has_side_effects=True),

time: 73 us -> 66.9 us (0.916)
  Pallas kernels: 69.9 us -> 63.9 us
    pallas_call x1, Pallas kernels: 39.4 us -> 33.4 us  [mlp_and_sum(): pl.pallas_call(mlp_kernel, out_shape=jax.ShapeDtypeStruct(x.shape, x.dtyp...]
where the time goes in v6:
time: 66.9 us; the launch traced here: 66.8 us
  Pallas kernels  63.9 us (96%)
  local copies, waits for them, and re-layouts  2.29 us (3%)
    pallas_call x1, Pallas kernels, mlp_and_sum(): pl.pallas_call(mlp_kernel, out_shape=jax.ShapeDtypeStruct(x.shape, x.dtyp...  33.4 us
    pallas_call x1, Pallas kernels, attend(): pl.pallas_call(attention_kernel, out_shape=[jax.ShapeDtypeStruct((rows *...  30.5 us
    unnamed x1, local copies, waits for them, and re-layouts  2.29 us

profile of v6, /device:TPU:113, one launch (start us, length us, event | category | flops | bytes accessed | tf_op | source)
XLA Modules:
  0.0 66.8 jit_solution(5448376828468434314)
XLA Ops:
  0.6 30.5 %attend.1 = (f32[512,128]{1,0:T(8,128)}, bf16[128,4,128,128]{3,2,1,0:T(8,128)(2,1)}, bf16[128,4,128,128]{3,2,1,0:T(8,128)(2,1)}) custom-call(s32[128]{0:T(128)} %pos_hbm.1, s32[1,128]{1,0:T(1,128)} %bitcast.15, bf16[128,4096]{1,0:T(8,128)(2,1)} %x_hbm.3, f32[32,128]{1,0:T(8,128)} %bitcast.11, f32[32,128]{1,0:T(8,128)} %bitcast.12, ...), custom_call_target="tpu_custom_call" | custom-call | tf_op jit(solution)/shard_map/attend/pallas_call | solution.py:195
  31.1 33.4 %mlp_and_sum.1 = bf16[128,4096]{1,0:T(8,128)(2,1)} custom-call(bf16[128,4096]{1,0:T(8,128)(2,1)} %x_hbm.3, f32[32,128]{1,0:T(8,128)} %bitcast.13, f32[32,128]{1,0:T(8,128)} %bitcast.14, f32[512,128]{1,0:T(8,128)} %get-tuple-element.6.ctx_hbm, bf16[512,4096]{1,0:T(8,128)(2,1)} %bitcast.10, bf16[4096,2048]{1,0:T(8,128)(2,1)} %wu_ref.1, bf16[2048,4096]{1,0:T(8,128)(2,1)} %wd_ref.1), custom_call_target="tpu_custom_call" | custom-call | tf_op jit(solution)/shard_map/mlp_and_sum/pallas_call | solution.py:374
  64.5 2.3 %copy.16 = bf16[128,4096]{1,0:T(8,128)(2,1)} copy(bf16[128,4096]{1,0:T(8,128)(2,1)} %mlp_and_sum.1) | data formatting | bytes 2097152

commit v7 on v6

--- a/solution.py
+++ b/solution.py
@@ -13,8 +13,8 @@
 LANES = 128
 ROWS_PER_CHUNK = 8
 W_CHUNK = 256
-W_AHEAD = 8
-KV_AHEAD = 6
+W_AHEAD = 16
+KV_AHEAD = 12
 UP_COLS = 256
 AHEAD = 2
 OUT_COLS = 512
@@ -226,7 +226,7 @@
 
 
 def mlp_kernel(x_hbm, gamma_hbm, beta_hbm, ctx_hbm, wo_ref, wu_ref, wd_ref, out_ref,
-               x_ref, gamma_ref, beta_ref, ctx_ref, small, wub, wcat, mlp_in, lhs, part, d2d_src, d2d_dst, cs32, csb, inbox, outb, usem, dsem, osem, send, recv, stored):
+               x_ref, gamma_ref, beta_ref, ctx_ref, small, wub, wcat, mlp_in, lhs, part, d2d_src, d2d_dst, cs32, csb, inbox, outb, usem, dsem, osem, send, recv):
     n_u, _, cu = wub.shape
     n_b, _, cb = wcat.shape
     half, slab = d2d_src.shape[1], inbox.shape[2]
@@ -341,13 +341,10 @@
             remote(kind, j).wait_recv()
             remote(kind + 4, j).start()
 
-    def store(j):
-        return pltpu.make_async_copy(outb.at[j], out_ref.at[:, pl.ds(j * cb, cb)], stored.at[j])
-
     def collect(j):
         for kind in (7, 8, 9, 10):
             remote(kind, j).wait_recv()
-        store(j).start()
+        out_ref[:, j * cb:(j + 1) * cb] = outb[j]
 
     stages = ((compute, 0.0), (chip_sum, 1.4), (finish, 5.0), (share, 8.6), (collect, 10.0))
     plan = sorted((j * BLOCK_US + after, n, j) for n, (_, after) in enumerate(stages) for j in range(n_b))
@@ -356,7 +353,6 @@
     for j in range(n_b):
         for kind in range(11):
             remote(kind, j).wait_send()
-        store(j).wait()
 
 
 def mlp_and_sum(mesh, x, gamma, beta, context, w_out, w_up, w_down):
@@ -375,7 +371,7 @@
         mlp_kernel,
         out_shape=jax.ShapeDtypeStruct(x.shape, x.dtype),
         in_specs=[HBM] * 7,
-        out_specs=HBM,
+        out_specs=pl.BlockSpec(memory_space=pltpu.VMEM),
         scratch_shapes=[
             pltpu.VMEM((rows, width), BF16),
             pltpu.VMEM((width // LANES, LANES), F32),
@@ -398,9 +394,8 @@
             pltpu.SemaphoreType.DMA((n_b,)),
             pltpu.SemaphoreType.DMA((11, n_b)),
             pltpu.SemaphoreType.DMA((11, n_b)),
-            pltpu.SemaphoreType.DMA((n_b,)),
         ],
-        compiler_params=pltpu.CompilerParams(vmem_limit_bytes=60 * 1024 * 1024, collective_id=0, has_side_effects=True),
+        compiler_params=pltpu.CompilerParams(vmem_limit_bytes=48 * 1024 * 1024, collective_id=0, has_side_effects=True),
         name='mlp_and_sum',
     )(x, gamma.reshape(-1, LANES), beta.reshape(-1, LANES), context, w_out, w_up, w_down)
 

time: 66.9 us -> 62.1 us (0.928)
  Pallas kernels: 63.9 us -> 59.3 us
    pallas_call x1, Pallas kernels: 30.5 us -> 28.1 us  [attend(): pl.pallas_call(attention_kernel, out_shape=[jax.ShapeDtypeStruct((rows *...]
    pallas_call x1, Pallas kernels: 33.4 us -> 31.2 us  [mlp_and_sum(): pl.pallas_call(mlp_kernel, out_shape=jax.ShapeDtypeStruct(x.shape, x.dtyp...]
    unnamed x1 -> x9, local copies, waits for them, and re-layouts: 2.29 us -> 1.93 us
where the time goes in v7:
time: 62.1 us; the launch traced here: 61.9 us
  Pallas kernels  59.3 us (95%)
  local copies, waits for them, and re-layouts  1.93 us (3%)
  between operations  0.7 us (1%)
    pallas_call x1, Pallas kernels, mlp_and_sum(): pl.pallas_call(mlp_kernel, out_shape=jax.ShapeDtypeStruct(x.shape, x.dtyp...  31.2 us
    pallas_call x1, Pallas kernels, attend(): pl.pallas_call(attention_kernel, out_shape=[jax.ShapeDtypeStruct((rows *...  28.1 us
    unnamed x9, local copies, waits for them, and re-layouts  1.93 us

profile of v7, /device:TPU:113, one launch (start us, length us, event | category | flops | bytes accessed | tf_op | source)
XLA Modules:
  0.0 61.9 jit_solution(18444037136021646179)
XLA Ops:
  0.6 0.0 copy-start
  0.6 0.0 copy-start.2
  0.7 0.0 copy-start.3
  0.7 28.1 %attend.1 = (f32[512,128]{1,0:T(8,128)}, bf16[128,4,128,128]{3,2,1,0:T(8,128)(2,1)}, bf16[128,4,128,128]{3,2,1,0:T(8,128)(2,1)}) custom-call(s32[128]{0:T(128)} %pos_hbm.1, s32[1,128]{1,0:T(1,128)} %bitcast.15, bf16[128,4096]{1,0:T(8,128)(2,1)} %x_hbm.3, f32[32,128]{1,0:T(8,128)} %bitcast.13, f32[32,128]{1,0:T(8,128)} %bitcast.14, ...), custom_call_target="tpu_custom_call" | custom-call | tf_op jit(solution)/shard_map/attend/pallas_call | solution.py:195
  28.8 0.0 copy-done
  28.8 0.0 copy-done.2
  28.8 0.0 copy-done.3
  28.8 0.0 copy-start.1
  28.9 0.9 %copy-done.1 = f32[512,128]{1,0:T(8,128)S(1)} copy-done((f32[512,128]{1,0:T(8,128)S(1)}, f32[512,128]{1,0:T(8,128)}, u32[]{:S(2)}) %copy-start.1) | copy-done | bytes 262168
  29.8 31.2 %mlp_and_sum.1 = bf16[128,4096]{1,0:T(8,128)(2,1)S(1)} custom-call(bf16[128,4096]{1,0:T(8,128)(2,1)S(1)} %copy-done, f32[32,128]{1,0:T(8,128)S(1)} %bitcast.9, f32[32,128]{1,0:T(8,128)S(1)} %bitcast.10, f32[512,128]{1,0:T(8,128)S(1)} %copy-done.1, bf16[512,4096]{1,0:T(8,128)(2,1)} %bitcast.12, bf16[4096,2048]{1,0:T(8,128)(2,1)} %wu_ref.1, ...), custom_call_target="tpu_custom_call" | custom-call | tf_op jit(solution)/shard_map/mlp_and_sum/pallas_call | solution.py:370
  61.0 1.0 %copy.16 = bf16[128,4096]{1,0:T(8,128)(2,1)} copy(bf16[128,4096]{1,0:T(8,128)(2,1)S(1)} %mlp_and_sum.1) | data formatting | bytes 2097152
Async XLA Ops:
  0.6 28.2 %copy-start = (bf16[128,4096]{1,0:T(8,128)(2,1)S(1)}, bf16[128,4096]{1,0:T(8,128)(2,1)}, u32[]{:S(2)}) copy-start(bf16[128,4096]{1,0:T(8,128)(2,1)} %x_hbm.3) | copy-start | bytes 3145732
  0.6 28.2 %copy-start.2 = (f32[4096]{0:T(1024)S(1)}, f32[4096]{0:T(1024)}, u32[]{:S(2)}) copy-start(f32[4096]{0:T(1024)} %param.15) | copy-start | bytes 49156
  0.7 28.2 %copy-start.3 = (f32[4096]{0:T(1024)S(1)}, f32[4096]{0:T(1024)}, u32[]{:S(2)}) copy-start(f32[4096]{0:T(1024)} %param.16) | copy-start | bytes 49156
  28.8 1.0 %copy-start.1 = (f32[512,128]{1,0:T(8,128)S(1)}, f32[512,128]{1,0:T(8,128)}, u32[]{:S(2)}) copy-start(f32[512,128]{1,0:T(8,128)} %get-tuple-element.6.ctx_hbm) | copy-start | bytes 786436

commit v8 on v7

--- a/solution.py
+++ b/solution.py
@@ -16,12 +16,13 @@
 W_AHEAD = 16
 KV_AHEAD = 12
 UP_COLS = 256
-AHEAD = 2
+AHEAD = 4
 OUT_COLS = 512
 BLOCK_US = 0.9
 F32 = jnp.float32
 BF16 = jnp.bfloat16
 HBM = pl.BlockSpec(memory_space=pltpu.HBM)
+VMEM = pl.BlockSpec(memory_space=pltpu.VMEM)
 MESH = pl.DeviceIdType.MESH
 
 
@@ -51,8 +52,8 @@
     lax.fori_loop(0, tiles, write, 0, unroll=4)
 
 
-def attention_kernel(pos_hbm, pos_row_hbm, x_hbm, gamma_hbm, beta_hbm, w_ref, k_ref, v_ref, ctx_hbm, ko_ref, vo_ref,
-                     pos_ref, pos_row, x_ref, gamma_ref, beta_ref, ctx_ref,
+def attention_kernel(pos_hbm, pos_row_hbm, x_hbm, gamma_hbm, beta_hbm, w_ref, k_ref, v_ref, ctx_ref, ko_ref, vo_ref,
+                     pos_ref, pos_row, x_ref, gamma_ref, beta_ref,
                      wbuf, wf, acc, attn, q_s, kn_s, vn_s, kbuf, vbuf, small, wsem, insem, outsem):
     rows, width = x_ref.shape
     _, groups, slots, head = k_ref.shape
@@ -178,12 +179,9 @@
         return carry
 
     lax.fori_loop(0, n_c, chunk, 0)
-    ctx_out = pltpu.make_async_copy(ctx_ref, ctx_hbm, small.at[0])
-    ctx_out.start()
     for i in range(n_c):
         io(i, 0, True).wait()
         io(i, 1, True).wait()
-    ctx_out.wait()
 
 
 def attend(x, gamma, beta, w_qkv, k_cache, v_cache, positions):
@@ -198,14 +196,13 @@
                    jax.ShapeDtypeStruct(k_cache.shape, k_cache.dtype),
                    jax.ShapeDtypeStruct(v_cache.shape, v_cache.dtype)],
         in_specs=[HBM] * 8,
-        out_specs=[HBM] * 3,
+        out_specs=[VMEM, HBM, HBM],
         scratch_shapes=[
             pltpu.SMEM((rows,), jnp.int32),
             pltpu.VMEM((1, rows), jnp.int32),
             pltpu.VMEM((rows, width), BF16),
             pltpu.VMEM((width // LANES, LANES), F32),
             pltpu.VMEM((width // LANES, LANES), F32),
-            pltpu.VMEM((rows * groups, head), F32),
             pltpu.VMEM((width * cols, head), BF16),
             pltpu.VMEM((W_CHUNK * cols, head), F32),
             pltpu.VMEM((rows, cols * head), F32),
@@ -220,13 +217,13 @@
             pltpu.SemaphoreType.DMA((2, n_c)),
             pltpu.SemaphoreType.DMA((2, n_c)),
         ],
-        compiler_params=pltpu.CompilerParams(vmem_limit_bytes=60 * 1024 * 1024),
+        compiler_params=pltpu.CompilerParams(vmem_limit_bytes=53 * 1024 * 1024),
         name='attend',
     )(positions, positions.reshape(1, rows), x, gamma.reshape(-1, LANES), beta.reshape(-1, LANES), w_rows, k_cache, v_cache)
 
 
-def mlp_kernel(x_hbm, gamma_hbm, beta_hbm, ctx_hbm, wo_ref, wu_ref, wd_ref, out_ref,
-               x_ref, gamma_ref, beta_ref, ctx_ref, small, wub, wcat, mlp_in, lhs, part, d2d_src, d2d_dst, cs32, csb, inbox, outb, usem, dsem, osem, send, recv):
+def mlp_kernel(x_hbm, gamma_hbm, beta_hbm, ctx_ref, wo_ref, wu_ref, wd_ref, out_ref,
+               x_ref, gamma_ref, beta_ref, small, wub, wcat, mlp_in, lhs, part, d2d_src, d2d_dst, cs32, csb, inbox, outb, usem, dsem, osem, send, recv):
     n_u, _, cu = wub.shape
     n_b, _, cb = wcat.shape
     half, slab = d2d_src.shape[1], inbox.shape[2]
@@ -259,7 +256,7 @@
             down_copy(n - n_u).start()
 
     first = [pltpu.make_async_copy(src, dst, small.at[n]) for n, (src, dst) in enumerate(
-        ((x_hbm, x_ref), (gamma_hbm, gamma_ref), (beta_hbm, beta_ref), (ctx_hbm, ctx_ref)))]
+        ((x_hbm, x_ref), (gamma_hbm, gamma_ref), (beta_hbm, beta_ref)))]
     for copy in first:
         copy.start()
     for n in range(AHEAD):
@@ -346,7 +343,7 @@
             remote(kind, j).wait_recv()
         out_ref[:, j * cb:(j + 1) * cb] = outb[j]
 
-    stages = ((compute, 0.0), (chip_sum, 1.4), (finish, 5.0), (share, 8.6), (collect, 10.0))
+    stages = ((compute, 0.0), (chip_sum, 1.6), (finish, 5.6), (share, 10.0), (collect, 11.6))
     plan = sorted((j * BLOCK_US + after, n, j) for n, (_, after) in enumerate(stages) for j in range(n_b))
     for _, n, j in plan:
         stages[n][0](j)
@@ -370,14 +367,13 @@
     return pl.pallas_call(
         mlp_kernel,
         out_shape=jax.ShapeDtypeStruct(x.shape, x.dtype),
-        in_specs=[HBM] * 7,
-        out_specs=pl.BlockSpec(memory_space=pltpu.VMEM),
+        in_specs=[HBM, HBM, HBM, VMEM, HBM, HBM, HBM],
+        out_specs=VMEM,
         scratch_shapes=[
             pltpu.VMEM((rows, width), BF16),
             pltpu.VMEM((width // LANES, LANES), F32),
             pltpu.VMEM((width // LANES, LANES), F32),
-            pltpu.VMEM(context.shape, F32),
-            pltpu.SemaphoreType.DMA((4,)),
+            pltpu.SemaphoreType.DMA((3,)),
             pltpu.VMEM((n_u, width, UP_COLS), BF16),
             block(BF16, ctx_width + hidden, OUT_COLS),
             pltpu.VMEM((rows, width), BF16),

time: 62.1 us -> 61.1 us (0.984)
  Pallas kernels: 59.3 us -> 57.1 us
  local copies, waits for them, and re-layouts: 1.93 us -> 3.07 us
    pallas_call x1, Pallas kernels: 31.2 us -> 29 us  [mlp_and_sum(): pl.pallas_call(mlp_kernel, out_shape=jax.ShapeDtypeStruct(x.shape, x.dtyp...]
    unnamed x9 -> x13, local copies, waits for them, and re-layouts: 1.93 us -> 3.07 us
where the time goes in v8:
time: 61.1 us; the launch traced here: 60.8 us
  Pallas kernels  57.1 us (93%)
  local copies, waits for them, and re-layouts  3.07 us (5%)
  between operations  0.68 us (1%)
    pallas_call x1, Pallas kernels, mlp_and_sum(): pl.pallas_call(mlp_kernel, out_shape=jax.ShapeDtypeStruct(x.shape, x.dtyp...  29 us
    pallas_call x1, Pallas kernels, attend(): pl.pallas_call(attention_kernel, out_shape=[jax.ShapeDtypeStruct((rows *...  28.1 us
    unnamed x13, local copies, waits for them, and re-layouts  3.07 us

profile of v8, /device:TPU:113, one launch (start us, length us, event | category | flops | bytes accessed | tf_op | source)
XLA Modules:
  0.0 60.8 jit_solution(4343481256381100218)
XLA Ops:
  0.6 0.0 copy-start.1
  0.6 0.7 %copy-done.1 = f32[4096]{0:T(1024)S(1)} copy-done((f32[4096]{0:T(1024)S(1)}, f32[4096]{0:T(1024)}, u32[]{:S(2)}) %copy-start.1) | copy-done | bytes 16408
  1.4 0.0 copy-start.2
  1.4 0.7 %copy-done.2 = f32[4096]{0:T(1024)S(1)} copy-done((f32[4096]{0:T(1024)S(1)}, f32[4096]{0:T(1024)}, u32[]{:S(2)}) %copy-start.2) | copy-done | bytes 16408
  2.1 0.0 copy-start.5
  2.1 0.7 %copy-done.5 = s32[128]{0:T(128)S(1)} copy-done((s32[128]{0:T(128)S(1)}, s32[128]{0:T(128)}, u32[]{:S(2)}) %copy-start.5) | copy-done | bytes 536
  2.7 0.0 copy-start
  2.7 0.0 copy-start.3
  2.7 0.0 copy-start.4
  2.7 28.1 %attend.1 = (f32[512,128]{1,0:T(8,128)S(1)}, bf16[128,4,128,128]{3,2,1,0:T(8,128)(2,1)}, bf16[128,4,128,128]{3,2,1,0:T(8,128)(2,1)}) custom-call(s32[128]{0:T(128)S(1)} %copy-done.5, s32[1,128]{1,0:T(1,128)S(1)} %bitcast.13, bf16[128,4096]{1,0:T(8,128)(2,1)} %x_hbm.3, f32[32,128]{1,0:T(8,128)S(1)} %bitcast.9, f32[32,128]{1,0:T(8,128)S(1)} %bitcast.10, ...), custom_call_target="tpu_custom_call" | custom-call | tf_op jit(solution)/shard_map/attend/pallas_call | solution.py:193
  30.8 0.0 copy-done
  30.8 0.0 copy-done.3
  30.8 0.0 copy-done.4
  30.8 29.0 %mlp_and_sum.1 = bf16[128,4096]{1,0:T(8,128)(2,1)S(1)} custom-call(bf16[128,4096]{1,0:T(8,128)(2,1)S(1)} %copy-done, f32[32,128]{1,0:T(8,128)S(1)} %bitcast.11, f32[32,128]{1,0:T(8,128)S(1)} %bitcast.12, f32[512,128]{1,0:T(8,128)S(1)} %get-tuple-element.6.ctx_ref, bf16[512,4096]{1,0:T(8,128)(2,1)} %bitcast.15, bf16[4096,2048]{1,0:T(8,128)(2,1)} %wu_ref.1, ...), custom_call_target="tpu_custom_call" | custom-call | tf_op jit(solution)/shard_map/mlp_and_sum/pallas_call | solution.py:367
  59.8 1.0 %copy.16 = bf16[128,4096]{1,0:T(8,128)(2,1)} copy(bf16[128,4096]{1,0:T(8,128)(2,1)S(1)} %mlp_and_sum.1) | data formatting | bytes 2097152
Async XLA Ops:
  0.6 0.7 %copy-start.1 = (f32[4096]{0:T(1024)S(1)}, f32[4096]{0:T(1024)}, u32[]{:S(2)}) copy-start(f32[4096]{0:T(1024)} %param.13) | copy-start | bytes 49156
  1.4 0.7 %copy-start.2 = (f32[4096]{0:T(1024)S(1)}, f32[4096]{0:T(1024)}, u32[]{:S(2)}) copy-start(f32[4096]{0:T(1024)} %param.14) | copy-start | bytes 49156
  2.1 0.7 %copy-start.5 = (s32[128]{0:T(128)S(1)}, s32[128]{0:T(128)}, u32[]{:S(2)}) copy-start(s32[128]{0:T(128)} %pos_hbm.1) | copy-start | bytes 1540
  2.7 28.1 %copy-start = (bf16[128,4096]{1,0:T(8,128)(2,1)S(1)}, bf16[128,4096]{1,0:T(8,128)(2,1)}, u32[]{:S(2)}) copy-start(bf16[128,4096]{1,0:T(8,128)(2,1)} %x_hbm.3) | copy-start | bytes 3145732
  2.7 28.1 %copy-start.3 = (f32[4096]{0:T(1024)S(1)}, f32[4096]{0:T(1024)}, u32[]{:S(2)}) copy-start(f32[4096]{0:T(1024)} %param.15) | copy-start | bytes 49156
  2.7 28.1 %copy-start.4 = (f32[4096]{0:T(1024)S(1)}, f32[4096]{0:T(1024)}, u32[]{:S(2)}) copy-start(f32[4096]{0:T(1024)} %param.16) | copy-start | bytes 49156

commit v9 on v8

--- a/solution.py
+++ b/solution.py
@@ -16,7 +16,7 @@
 W_AHEAD = 16
 KV_AHEAD = 12
 UP_COLS = 256
-AHEAD = 4
+AHEAD = 6
 OUT_COLS = 512
 BLOCK_US = 0.9
 F32 = jnp.float32
@@ -219,7 +219,8 @@
         ],
         compiler_params=pltpu.CompilerParams(vmem_limit_bytes=53 * 1024 * 1024),
         name='attend',
-    )(positions, positions.reshape(1, rows), x, gamma.reshape(-1, LANES), beta.reshape(-1, LANES), w_rows, k_cache, v_cache)
+    )(*(pltpu.with_memory_space_constraint(a, pltpu.HBM) for a in (
+        positions, positions.reshape(1, rows), x, gamma.reshape(-1, LANES), beta.reshape(-1, LANES))), w_rows, k_cache, v_cache)
 
 
 def mlp_kernel(x_hbm, gamma_hbm, beta_hbm, ctx_ref, wo_ref, wu_ref, wd_ref, out_ref,
@@ -343,7 +344,7 @@
             remote(kind, j).wait_recv()
         out_ref[:, j * cb:(j + 1) * cb] = outb[j]
 
-    stages = ((compute, 0.0), (chip_sum, 1.6), (finish, 5.6), (share, 10.0), (collect, 11.6))
+    stages = ((compute, 0.0), (chip_sum, 1.6), (finish, 6.4), (share, 11.2), (collect, 12.8))
     plan = sorted((j * BLOCK_US + after, n, j) for n, (_, after) in enumerate(stages) for j in range(n_b))
     for _, n, j in plan:
         stages[n][0](j)

time: 61.1 us -> 58.8 us (0.962)
  local copies, waits for them, and re-layouts: 3.07 us -> 0.99 us
    unnamed x13 -> x7, local copies, waits for them, and re-layouts: 3.07 us -> 0.99 us
where the time goes in v9:
time: 58.8 us; the launch traced here: 58.7 us
  Pallas kernels  57 us (97%)
  local copies, waits for them, and re-layouts  0.99 us (2%)
  between operations  0.7 us (1%)
    pallas_call x1, Pallas kernels, mlp_and_sum(): pl.pallas_call(mlp_kernel, out_shape=jax.ShapeDtypeStruct(x.shape, x.dtyp...  28.9 us
    pallas_call x1, Pallas kernels, attend(): pl.pallas_call(attention_kernel, out_shape=[jax.ShapeDtypeStruct((rows *...  28.1 us

profile of v9, /device:TPU:113, one launch (start us, length us, event | category | flops | bytes accessed | tf_op | source)
XLA Modules:
  0.0 58.7 jit_solution(14044563682320492714)
XLA Ops:
  0.6 0.0 copy-start
  0.6 0.0 copy-start.1
  0.7 0.0 copy-start.2
  0.7 28.1 %attend.1 = (f32[512,128]{1,0:T(8,128)S(1)}, bf16[128,4,128,128]{3,2,1,0:T(8,128)(2,1)}, bf16[128,4,128,128]{3,2,1,0:T(8,128)(2,1)}) custom-call(s32[128]{0:T(128)} %pos_hbm.1, s32[1,128]{1,0:T(1,128)} %bitcast.15, bf16[128,4096]{1,0:T(8,128)(2,1)} %x_hbm.3, f32[32,128]{1,0:T(8,128)} %bitcast.13, f32[32,128]{1,0:T(8,128)} %bitcast.14, ...), custom_call_target="tpu_custom_call" | custom-call | tf_op jit(solution)/shard_map/attend/pallas_call | solution.py:193
  28.7 0.0 copy-done
  28.8 0.0 copy-done.1
  28.8 0.0 copy-done.2
  28.8 28.9 %mlp_and_sum.1 = bf16[128,4096]{1,0:T(8,128)(2,1)S(1)} custom-call(bf16[128,4096]{1,0:T(8,128)(2,1)S(1)} %copy-done, f32[32,128]{1,0:T(8,128)S(1)} %bitcast.9, f32[32,128]{1,0:T(8,128)S(1)} %bitcast.10, f32[512,128]{1,0:T(8,128)S(1)} %get-tuple-element.6.ctx_ref, bf16[512,4096]{1,0:T(8,128)(2,1)} %bitcast.12, bf16[4096,2048]{1,0:T(8,128)(2,1)} %wu_ref.1, ...), custom_call_target="tpu_custom_call" | custom-call | tf_op jit(solution)/shard_map/mlp_and_sum/pallas_call | solution.py:368
  57.7 1.0 %copy.16 = bf16[128,4096]{1,0:T(8,128)(2,1)} copy(bf16[128,4096]{1,0:T(8,128)(2,1)S(1)} %mlp_and_sum.1) | data formatting | bytes 2097152
Async XLA Ops:
  0.6 28.1 %copy-start = (bf16[128,4096]{1,0:T(8,128)(2,1)S(1)}, bf16[128,4096]{1,0:T(8,128)(2,1)}, u32[]{:S(2)}) copy-start(bf16[128,4096]{1,0:T(8,128)(2,1)} %x_hbm.3) | copy-start | bytes 3145732
  0.6 28.1 %copy-start.1 = (f32[4096]{0:T(1024)S(1)}, f32[4096]{0:T(1024)}, u32[]{:S(2)}) copy-start(f32[4096]{0:T(1024)} %param.15) | copy-start | bytes 49156
  0.7 28.1 %copy-start.2 = (f32[4096]{0:T(1024)S(1)}, f32[4096]{0:T(1024)}, u32[]{:S(2)}) copy-start(f32[4096]{0:T(1024)} %param.16) | copy-start | bytes 49156

commit v10 on v9

--- a/solution.py
+++ b/solution.py
@@ -344,7 +344,7 @@
             remote(kind, j).wait_recv()
         out_ref[:, j * cb:(j + 1) * cb] = outb[j]
 
-    stages = ((compute, 0.0), (chip_sum, 1.6), (finish, 6.4), (share, 11.2), (collect, 12.8))
+    stages = ((compute, 0.0), (chip_sum, 1.3), (finish, 4.2), (share, 7.8), (collect, 9.0))
     plan = sorted((j * BLOCK_US + after, n, j) for n, (_, after) in enumerate(stages) for j in range(n_b))
     for _, n, j in plan:
         stages[n][0](j)

time: 58.8 us -> 60.2 us (1.024)
  Pallas kernels: 57 us -> 58.4 us
    pallas_call x1, Pallas kernels: 28.9 us -> 30.3 us  [mlp_and_sum(): pl.pallas_call(mlp_kernel, out_shape=jax.ShapeDtypeStruct(x.shape, x.dtyp...]
where the time goes in v10:
time: 60.2 us; the launch traced here: 60.1 us
  Pallas kernels  58.4 us (97%)
  local copies, waits for them, and re-layouts  0.99 us (2%)
  between operations  0.7 us (1%)
    pallas_call x1, Pallas kernels, mlp_and_sum(): pl.pallas_call(mlp_kernel, out_shape=jax.ShapeDtypeStruct(x.shape, x.dtyp...  30.3 us
    pallas_call x1, Pallas kernels, attend(): pl.pallas_call(attention_kernel, out_shape=[jax.ShapeDtypeStruct((rows *...  28.1 us

profile of v10, /device:TPU:113, one launch (start us, length us, event | category | flops | bytes accessed | tf_op | source)
XLA Modules:
  0.0 60.1 jit_solution(10905319960843149571)
XLA Ops:
  0.6 0.0 copy-start
  0.6 0.0 copy-start.1
  0.7 0.0 copy-start.2
  0.7 28.1 %attend.1 = (f32[512,128]{1,0:T(8,128)S(1)}, bf16[128,4,128,128]{3,2,1,0:T(8,128)(2,1)}, bf16[128,4,128,128]{3,2,1,0:T(8,128)(2,1)}) custom-call(s32[128]{0:T(128)} %pos_hbm.1, s32[1,128]{1,0:T(1,128)} %bitcast.15, bf16[128,4096]{1,0:T(8,128)(2,1)} %x_hbm.3, f32[32,128]{1,0:T(8,128)} %bitcast.13, f32[32,128]{1,0:T(8,128)} %bitcast.14, ...), custom_call_target="tpu_custom_call" | custom-call | tf_op jit(solution)/shard_map/attend/pallas_call | solution.py:193
  28.7 0.0 copy-done
  28.8 0.0 copy-done.1
  28.8 0.0 copy-done.2
  28.8 30.3 %mlp_and_sum.1 = bf16[128,4096]{1,0:T(8,128)(2,1)S(1)} custom-call(bf16[128,4096]{1,0:T(8,128)(2,1)S(1)} %copy-done, f32[32,128]{1,0:T(8,128)S(1)} %bitcast.9, f32[32,128]{1,0:T(8,128)S(1)} %bitcast.10, f32[512,128]{1,0:T(8,128)S(1)} %get-tuple-element.6.ctx_ref, bf16[512,4096]{1,0:T(8,128)(2,1)} %bitcast.12, bf16[4096,2048]{1,0:T(8,128)(2,1)} %wu_ref.1, ...), custom_call_target="tpu_custom_call" | custom-call | tf_op jit(solution)/shard_map/mlp_and_sum/pallas_call | solution.py:368
  59.1 1.0 %copy.16 = bf16[128,4096]{1,0:T(8,128)(2,1)} copy(bf16[128,4096]{1,0:T(8,128)(2,1)S(1)} %mlp_and_sum.1) | data formatting | bytes 2097152
Async XLA Ops:
  0.6 28.1 %copy-start = (bf16[128,4096]{1,0:T(8,128)(2,1)S(1)}, bf16[128,4096]{1,0:T(8,128)(2,1)}, u32[]{:S(2)}) copy-start(bf16[128,4096]{1,0:T(8,128)(2,1)} %x_hbm.3) | copy-start | bytes 3145732
  0.6 28.1 %copy-start.1 = (f32[4096]{0:T(1024)S(1)}, f32[4096]{0:T(1024)}, u32[]{:S(2)}) copy-start(f32[4096]{0:T(1024)} %param.15) | copy-start | bytes 49156
  0.7 28.1 %copy-start.2 = (f32[4096]{0:T(1024)S(1)}, f32[4096]{0:T(1024)}, u32[]{:S(2)}) copy-start(f32[4096]{0:T(1024)} %param.16) | copy-start | bytes 49156
